TPU v7x, 32 devices: a whole 2x2x4 slice. The times are simulated.
32 devices in a mesh: pair: 8 (over z, x), aux: 4 (over y, core).
Axes of the slice: x: 2, y: 2, z: 4, core: 2. Of those that a mesh axis runs over, the one named last changes fastest.
Arguments:
- panels: bfloat16 [16, 120, 9216], P('pair', None, 'aux'), may hold values from -1.5 to 1.5
- amplitudes: bfloat16 [16, 2, 120, 120], P('pair'), may hold values from -0.5 to 0.5
- drive: float32 [16, 2, 14400], P('pair', None, 'aux'), may hold values from -6 to 6
- pno_energy: float32 [16, 120], P('pair'), may hold values from 1 to 3
- occ_energy: float32 [32], replicated, may hold values from -2 to -0.5
- frequency: float32 [1], replicated, may hold values from 0.2 to 2
- pair_lmo: int32 [16, 2], replicated, may hold values from 0 to 31
- neighbours: int32 [16, 8], P('pair'), may hold values from 0 to 15
- pno_ranks: int32 [16], P('pair'), may hold values from 60 to 120
- fock_off: float32 [32, 32], replicated, may hold values from -1.8 to 1.8
Outputs:
- residual: float32 [16, 2, 14400], P('pair', None, 'aux')
Inputs may be any that keep to these rules, and one draw needn't show every extreme that they name: `neighbours`: neighbour pairs; a pair may be listed more than once and may list itself. `pno_ranks`: rows of a pair's panel from its rank on are padding.
All inputs are finite; a program needn't handle non-finite values.
Results may differ from a plain program's by a relative error of at most 0.0033.
Values may be sent and summed in bfloat16 or wider, within the bound.
A program may use at most 128 MiB of HBM per device.

v0:
```python
import functools

import jax
import jax.numpy as jnp
from jax import lax
from jax.experimental import pallas as pl
from jax.experimental.pallas import tpu as pltpu
from jax.sharding import PartitionSpec as P

LANE = 128


def pair_weights(pair_lmo, neighbours, fock_off, first_pair):
    local_pairs = neighbours.shape[0]
    total_pairs = pair_lmo.shape[0]
    lmo_count = fock_off.shape[0]
    lmo_ids = jnp.arange(lmo_count, dtype=jnp.int32)
    own_lmo = lax.dynamic_slice_in_dim(pair_lmo, first_pair, local_pairs, 0)
    own_table = (own_lmo[:, :, None] == lmo_ids[None, None, :]).astype(jnp.float32)
    lmo_table = (pair_lmo[:, :, None] == lmo_ids[None, None, :]).astype(jnp.float32)
    pair_ids = jnp.arange(total_pairs, dtype=jnp.int32)
    onehot = (neighbours[:, :, None] == pair_ids[None, None, :]).astype(jnp.float32)
    fock_rows = jnp.einsum("psl,lm->psm", own_table, fock_off, precision=lax.Precision.HIGHEST)
    near_table = jnp.einsum("pkn,nsl->pksl", onehot, lmo_table)
    values = jnp.sum(fock_rows[:, None, :, :] * near_table, axis=(2, 3))
    weights = jnp.sum(values[:, :, None] * onehot, axis=1).astype(jnp.bfloat16)
    return (weights, own_table)


def plain_body(
    panels,
    amplitudes,
    drive,
    pno_energy,
    occ_energy,
    frequency,
    pair_lmo,
    neighbours,
    pno_ranks,
    fock_off,
):
    local_pairs, rank_dim, aux_width = panels.shape
    total_pairs = pair_lmo.shape[0]
    n_pair = lax.axis_size("pair")
    n_aux = lax.axis_size("aux")
    first_pair = lax.axis_index("pair") * local_pairs
    rows_index = jnp.arange(rank_dim, dtype=jnp.int32)
    keep_rows = rows_index[None, :] < pno_ranks[:, None]
    weights, own_table = pair_weights(pair_lmo, neighbours, fock_off, first_pair)
    weights = lax.all_gather(weights, "pair", axis=0, tiled=True)
    amps = jnp.where(keep_rows[:, :, None, None], jnp.transpose(amplitudes, (0, 2, 1, 3)), 0)
    amps = lax.all_gather(
        amps.reshape(local_pairs * rank_dim, 2 * rank_dim), "pair", axis=0, tiled=True
    )
    masked = jnp.where(keep_rows[:, :, None], panels, jnp.zeros_like(panels))
    slices = lax.all_to_all(
        masked.reshape(local_pairs * rank_dim, aux_width), "pair", 1, 0, tiled=True
    )
    products = jnp.einsum("iq,jq->ij", slices, slices, preferred_element_type=jnp.float32)
    products = products.reshape(total_pairs, rank_dim, total_pairs, rank_dim)
    mixed = (products * weights.astype(jnp.float32)[:, None, :, None]).astype(jnp.bfloat16)
    mixed = mixed.reshape(total_pairs * rank_dim, total_pairs * rank_dim)
    coupled = jnp.dot(mixed, amps, preferred_element_type=jnp.float32).astype(jnp.bfloat16)
    share_width = drive.shape[2]
    coupled = coupled.reshape(total_pairs, rank_dim, 2, rank_dim).transpose(0, 2, 1, 3)
    coupled = coupled.reshape(n_pair, local_pairs, 2, n_aux, share_width).transpose(0, 3, 1, 2, 4)
    coupled = coupled.reshape(n_pair * n_aux, local_pairs, 2, share_width)
    coupled = lax.all_to_all(coupled, ("pair", "aux"), 0, 0, tiled=True)
    coupled_share = jnp.sum(coupled.astype(jnp.float32), axis=0)
    share_start = lax.axis_index("aux") * share_width
    occ_pair = jnp.sum(own_table * occ_energy[None, None, :], axis=(1, 2))
    shift = pno_energy[:, :, None] + pno_energy[:, None, :] - occ_pair[:, None, None]
    shift_flat = lax.dynamic_slice_in_dim(
        shift.reshape(local_pairs, rank_dim * rank_dim), share_start, share_width, 1
    )
    signs = jnp.array([1.0, -1.0], jnp.float32)
    factor = shift_flat[:, None, :] - signs[None, :, None] * frequency[0]
    amp_flat = amplitudes.reshape(local_pairs, 2, rank_dim * rank_dim)
    amp_share = lax.dynamic_slice_in_dim(amp_flat, share_start, share_width, 2).astype(jnp.float32)
    return drive + factor * amp_share + coupled_share


def remote(src, dst, send_sem, recv_sem, pair, aux):
    return pltpu.make_async_remote_copy(
        src_ref=src,
        dst_ref=dst,
        send_sem=send_sem,
        recv_sem=recv_sem,
        device_id=(pair, aux),
        device_id_type=pl.DeviceIdType.MESH,
    )


def kernel(
    n_pair, n_aux, rank, x_ref, a_ref, w_ref, out_ref,
    xb, ab, wb, wt, left_rows, acc, parts, parts_in, sums, sums_in,
    local_sem, x_send, x_recv, e_send, e_recv, f_send, f_recv, g_send, g_recv,
    a_send, a_recv, b_send, b_recv, w_send, w_recv, y_send, y_recv, z_send, z_recv,
):
    me = lax.axis_index("pair")
    aux = lax.axis_index("aux")
    core = lax.rem(aux, 2)
    chip = aux // 2
    mate = aux + 1 - 2 * core
    n_chip = n_aux // 2
    block = 2 * rank
    tiles = x_ref.shape[1] // LANE
    base = (tiles // n_pair) * LANE
    extra = tiles % n_pair
    stride = n_pair // (2 * extra) if extra else 1
    share = a_ref.shape[0] // n_aux
    quarter = rank // n_aux
    padded = parts.shape[2] // 2

    barrier = pltpu.get_barrier_semaphore()

    def greet(pair, other):
        pl.semaphore_signal(
            barrier, inc=1, device_id=(pair, other), device_id_type=pl.DeviceIdType.MESH
        )

    for t in range(1, n_pair):
        peer = lax.rem(me + t, n_pair)
        greet(peer, aux)
        greet(peer, mate)
    for t in range(1, n_aux):
        greet(me, lax.rem(aux + t, n_aux))
    pl.semaphore_wait(barrier, 2 * (n_pair - 1) + n_aux - 1)

    def holder(which, level):
        spot = 2 * level + which
        shift = spot % 2 if not hasattr(spot, "dtype") else lax.rem(spot, 2)
        return stride * spot + (shift if stride > 1 else 0)

    lanes = pl.ds(pl.multiple_of(core * base, LANE), base)
    mate_lanes = pl.ds(pl.multiple_of((1 - core) * base, LANE), base)
    extra_lanes = pl.ds(2 * base, LANE)
    my_share = pl.ds(pl.multiple_of(aux * share, 16), share)

    def own_cols(peer):
        return x_ref.at[:, pl.ds(pl.multiple_of(peer * base, LANE), base)]

    half = n_pair // 2
    near = (me // half) * half
    far = half - near
    across = lax.rem(me + half, n_pair)

    def near_peer(t):
        return near + lax.rem(me - near + t, half)

    def far_peer(t):
        return far + lax.rem(me - near + t, half)

    def send_a(t):
        peer = near_peer(t) if t else across
        return remote(a_ref.at[my_share], ab.at[me, my_share], a_send.at[t], a_recv.at[me], peer, aux)

    def pass_a(t):
        rows = ab.at[across, my_share]
        return remote(rows, rows, a_send.at[half + t], a_recv.at[across], near_peer(t), aux)

    def wait_a(j):
        remote(
            a_ref.at[my_share], ab.at[j, my_share], a_send.at[0], a_recv.at[j], me, mate
        ).wait_recv()

    def send_w(t):
        peer = lax.rem(me + t, n_pair)
        return remote(w_ref, wb.at[me], w_send.at[t], w_recv.at[me], peer, aux)

    def send_x(peer):
        return remote(
            own_cols(peer), xb.at[me, :, lanes], x_send.at[peer], x_recv.at[me], peer, aux
        )

    def wait_x(j):
        remote(
            own_cols(me), xb.at[j, :, lanes], x_send.at[j], x_recv.at[j], me, mate
        ).wait_recv()

    def wait_f(j):
        remote(
            own_cols(me), xb.at[j, :, mate_lanes], f_send.at[j], f_recv.at[j], me, mate
        ).wait_recv()

    def extra_cols(level):
        return x_ref.at[:, pl.ds(base * n_pair + level * LANE, LANE)]

    def send_e(level):
        return remote(
            extra_cols(level), xb.at[me, :, extra_lanes], e_send.at[level], e_recv.at[me],
            holder(core, level), aux,
        )

    def send_f(j):
        return remote(xb.at[j, :, lanes], xb.at[j, :, lanes], f_send.at[j], f_recv.at[j], me, mate)

    def own_f():
        return remote(own_cols(me), xb.at[me, :, lanes], f_send.at[me], f_recv.at[me], me, mate)

    def send_g(j):
        return remote(
            xb.at[j, :, extra_lanes], xb.at[j, :, extra_lanes], g_send.at[j], g_recv.at[j], me, mate
        )

    def send_b(j, u):
        rows = ab.at[j, my_share]
        return remote(rows, rows, b_send.at[j, u], b_recv.at[aux, j], me, lax.rem(aux + u, n_aux))

    mine_x = pltpu.make_async_copy(own_cols(me), xb.at[me, :, lanes], local_sem.at[0])
    mine_a = pltpu.make_async_copy(a_ref, ab.at[me], local_sem.at[1])
    mine_w = pltpu.make_async_copy(w_ref, wb.at[me], local_sem.at[2])
    for t in range(half):
        send_a(t).start()
    for t in range(1, n_pair):
        send_w(t).start()
    for level in range(extra):
        @pl.when(holder(core, level) != me)
        def _():
            send_e(level).start()

        @pl.when(holder(core, level) == me)
        def _():
            pltpu.make_async_copy(
                extra_cols(level), xb.at[me, :, extra_lanes], local_sem.at[3]
            ).start()
    for t in range(half):
        send_x(far_peer(t)).start()
    own_f().start()
    mine_x.start()
    mine_a.start()
    mine_w.start()
    acc[...] = jnp.zeros_like(acc)

    def holds(which):
        found = me < 0
        for level in range(extra):
            found = jnp.logical_or(found, holder(which, level) == me)
        return found

    self_holds = holds(core)
    mate_holds = holds(1 - core)
    if extra:
        @pl.when(jnp.logical_not(jnp.logical_or(self_holds, mate_holds)))
        def _():
            xb[:, :, 2 * base :] = jnp.zeros((n_pair, block, LANE), xb.dtype)

    wait_a(across)
    for t in range(1, half):
        pass_a(t).start()
    for t in range(1, half):
        send_x(near_peer(t)).start()
    for t in range(half):
        arrived = [far_peer(t)] if t == 0 else [near_peer(half - t), far_peer(half - t)]
        for j in arrived:
            if t:
                wait_a(j)
            for u in range(1, n_aux):
                send_b(j, u).start()
    mine_x.wait()
    mine_a.wait()
    mine_w.wait()
    if extra:
        @pl.when(self_holds)
        def _():
            pltpu.make_async_copy(
                extra_cols(0), xb.at[me, :, extra_lanes], local_sem.at[3]
            ).wait()
            send_g(me).start()
            for t in range(1, n_pair):
                j = lax.rem(me + n_pair - t, n_pair)
                remote(
                    extra_cols(0), xb.at[j, :, extra_lanes], e_send.at[0], e_recv.at[j], me, mate
                ).wait_recv()
                send_g(j).start()

        @pl.when(mate_holds)
        def _():
            for j in range(n_pair):
                send_g(j).wait_recv()
    for t in range(1, half):
        j = near_peer(half - t)
        wait_x(j)
        send_f(j).start()
    for t in range(1, n_pair):
        j = lax.rem(me + n_pair - t, n_pair)
        remote(w_ref, wb.at[j], w_send.at[t], w_recv.at[j], me, mate).wait_recv()
        for u in range(1, n_aux):
            other = lax.rem(aux + u, n_aux)
            rows = ab.at[j, pl.ds(pl.multiple_of(other * share, 16), share)]
            remote(rows, rows, b_send.at[j, u], b_recv.at[other, j], me, other).wait_recv()
    table = wb[...]
    table = jnp.where(core == 0, table[:, 0], table[:, 1]).astype(jnp.bfloat16)
    pair_row = lax.broadcasted_iota(jnp.int32, (LANE, block), 0)
    column = lax.broadcasted_iota(jnp.int32, (LANE, block), 1)
    for j in range(n_pair):
        pick = pair_row == jnp.where(column < rank, 2 * j, 2 * j + 1)
        pick = jnp.where(pick, 1.0, 0.0).astype(jnp.bfloat16)
        wt[j] = jnp.dot(table, pick, preferred_element_type=jnp.float32)

    def collect_rows(start):
        for side in range(2):
            @pl.when(core == side)
            def _():
                for i in range(half):
                    left_rows[start + i] = xb[start + i, side * rank : (side + 1) * rank, :]

    def couple(start, j):
        rows = jnp.concatenate([left_rows[start + i] for i in range(half)], axis=0)
        products = lax.dot_general(
            rows, xb[j], (((1,), (1,)), ((), ())), preferred_element_type=jnp.float32
        )
        scaled = [
            products[i * rank : (i + 1) * rank] * wt[j, pl.ds(start + i, 1), :]
            for i in range(half)
        ]
        mixed = jnp.concatenate(scaled, axis=0).astype(jnp.bfloat16)
        turn = jnp.dot(mixed, ab[j, :block, :], preferred_element_type=jnp.float32)
        for i in range(half):
            acc[start + i, :rank, :] += turn[i * rank : (i + 1) * rank]

    for t in range(half):
        wait_f(near_peer(t))
    collect_rows(near)

    def near_near(t, carry):
        couple(near, near + t)
        return carry

    lax.fori_loop(0, half, near_near, 0)

    def near_far(t, carry):
        j = far_peer(lax.rem(half - t, half))
        wait_x(j)
        send_f(j).start()
        wait_f(j)
        couple(near, j)
        return carry

    lax.fori_loop(0, half, near_far, 0)

    def far_all(j, carry):
        couple(far, j)
        return carry

    def send_y(i, u):
        other = lax.rem(chip + u, n_chip)
        return remote(
            parts.at[other, i], parts_in.at[u, i], y_send.at[u, i], y_recv.at[u, i],
            me, 2 * other + core,
        )

    def turn_pair(t):
        side = jnp.where(t < half, near, far)
        return side + lax.rem(me - near + 1 + t, half)

    def spread(t, carry):
        i = turn_pair(t)
        for k in range(n_aux):
            rows = acc[i, pl.ds(quarter * k, padded), :]
            parts[k // 2, i, pl.ds((k % 2) * padded, padded), :] = rows.astype(parts.dtype)
        for u in range(1, n_chip):
            send_y(i, u).start()
        return carry

    lax.fori_loop(0, half, spread, 0)
    collect_rows(far)
    lax.fori_loop(0, n_pair, far_all, 0)
    lax.fori_loop(half, n_pair, spread, 0)

    def send_z(i, to_core):
        return remote(
            sums.at[i, pl.ds(pl.multiple_of(to_core * padded, padded), padded)],
            sums_in.at[me, core], z_send.at[i, to_core], z_recv.at[me, core],
            i, 2 * chip + to_core,
        )

    def gather_sum(t, carry):
        i = turn_pair(t)
        total = parts[chip, i].astype(jnp.float32)
        for u in range(1, n_chip):
            send_y(i, u).wait_recv()
            total = total + parts_in[u, i].astype(jnp.float32)
        sums[i] = total.astype(sums.dtype)

        @pl.when(i != me)
        def _():
            send_z(i, core).start()

        send_z(i, 1 - core).start()
        return carry

    lax.fori_loop(0, n_pair, gather_sum, 0)
    sums_in[me, core] = sums[me, pl.ds(pl.multiple_of(core * padded, padded), padded), :]

    def arrive(j, from_core):
        remote(
            sums.at[j, pl.ds(0, padded)], sums_in.at[j, from_core],
            z_send.at[j, 0], z_recv.at[j, from_core], me, mate,
        ).wait_recv()

    for t in range(n_pair):
        j = lax.rem(me + n_pair - t, n_pair)
        if t:
            arrive(j, core)
        arrive(j, 1 - core)
    for side in range(2):
        total = sums_in[0, side].astype(jnp.float32)
        for j in range(1, n_pair):
            total = total + sums_in[j, side].astype(jnp.float32)
        out_ref[side] = total

    for t in range(half):
        send_a(t).wait_send()
        send_x(far_peer(t)).wait_send()
        if t:
            pass_a(t).wait_send()
            send_x(near_peer(t)).wait_send()
    for t in range(1, n_pair):
        send_w(t).wait_send()
        j = lax.rem(me + n_pair - t, n_pair)
        send_f(j).wait_send()
        for u in range(1, n_aux):
            send_b(j, u).wait_send()
    own_f().wait_send()
    for level in range(extra):
        @pl.when(holder(core, level) != me)
        def _():
            send_e(level).wait_send()
    if extra:
        @pl.when(self_holds)
        def _():
            for j in range(n_pair):
                send_g(j).wait_send()

    def drain(i, carry):
        for u in range(1, n_chip):
            send_y(i, u).wait_send()

        @pl.when(i != me)
        def _():
            send_z(i, core).wait_send()

        send_z(i, 1 - core).wait_send()
        return carry

    lax.fori_loop(0, n_pair, drain, 0)


def fused_coupling(x_own, a_own, w_own, n_pair, n_aux, rank):
    block = 2 * rank
    tiles = x_own.shape[1] // LANE
    depth = 2 * (tiles // n_pair) * LANE + (LANE if tiles % n_pair else 0)
    n_chip = n_aux // 2
    extra = max(tiles % n_pair, 1)
    padded = -(-(rank // n_aux) // 16) * 16
    tall = -(-(rank - rank // n_aux + padded) // 8) * 8
    dma = pltpu.SemaphoreType.DMA
    bf16 = jnp.bfloat16
    return pl.pallas_call(
        functools.partial(kernel, n_pair, n_aux, rank),
        out_shape=jax.ShapeDtypeStruct((2, padded, block), jnp.float32),
        in_specs=[pl.BlockSpec(memory_space=pltpu.VMEM)] * 3,
        out_specs=pl.BlockSpec(memory_space=pltpu.VMEM),
        scratch_shapes=[
            pltpu.VMEM((n_pair, block, depth), bf16),
            pltpu.VMEM((n_pair,) + a_own.shape, bf16),
            pltpu.VMEM((n_pair,) + w_own.shape, jnp.float32),
            pltpu.VMEM((n_pair, n_pair, block), jnp.float32),
            pltpu.VMEM((n_pair, rank, depth), bf16),
            pltpu.VMEM((n_pair, tall, block), jnp.float32),
            pltpu.VMEM((n_chip, n_pair, 2 * padded, block), bf16),
            pltpu.VMEM((n_chip, n_pair, 2 * padded, block), bf16),
            pltpu.VMEM((n_pair, 2 * padded, block), bf16),
            pltpu.VMEM((n_pair, 2, padded, block), bf16),
            dma((4,)),
            dma((n_pair,)), dma((n_pair,)),
            dma((extra,)), dma((n_pair,)),
            dma((n_pair,)), dma((n_pair,)),
            dma((n_pair,)), dma((n_pair,)),
            dma((n_pair,)), dma((n_pair,)),
            dma((n_pair, n_aux)), dma((n_aux, n_pair)),
            dma((n_pair,)), dma((n_pair,)),
            dma((n_chip, n_pair)), dma((n_chip, n_pair)),
            dma((n_pair, 2)), dma((n_pair, 2)),
        ],
        compiler_params=pltpu.CompilerParams(collective_id=0, has_side_effects=True),
    )(x_own, a_own, w_own)


def fits(panels, n_pair, n_aux):
    local_pairs, rank, width = panels.shape
    tiles = width // LANE
    extra = tiles % n_pair
    return (
        local_pairs == 2
        and width % LANE == 0
        and rank % 8 == 0
        and rank % n_aux == 0
        and n_aux % 2 == 0
        and n_pair % 2 == 0
        and 2 * n_pair <= LANE
        and tiles >= n_pair
        and (extra == 0 or n_pair % (2 * extra) == 0)
    )


def body(*operands):
    if fits(operands[0], lax.axis_size("pair"), lax.axis_size("aux")):
        return kernel_body(*operands)
    return plain_body(*operands)


def kernel_body(
    panels,
    amplitudes,
    drive,
    pno_energy,
    occ_energy,
    frequency,
    pair_lmo,
    neighbours,
    pno_ranks,
    fock_off,
):
    local_pairs, rank_dim, aux_width = panels.shape
    n_pair = lax.axis_size("pair")
    n_aux = lax.axis_size("aux")
    first_pair = lax.axis_index("pair") * local_pairs
    rows_index = jnp.arange(rank_dim, dtype=jnp.int32)
    keep_rows = rows_index[None, :] < pno_ranks[:, None]
    weights, own_table = pair_weights(pair_lmo, neighbours, fock_off, first_pair)
    w_own = jnp.pad(weights.astype(jnp.float32), ((0, 0), (0, LANE - weights.shape[1])))
    amps = jnp.where(keep_rows[:, :, None, None], jnp.transpose(amplitudes, (0, 2, 1, 3)), 0)
    amps = amps.reshape(2 * rank_dim, 2 * rank_dim)
    tall = -(-2 * rank_dim // (16 * n_aux)) * 16 * n_aux
    amps = jnp.pad(amps, ((0, tall - 2 * rank_dim), (0, 0)))
    sums = fused_coupling(
        panels.reshape(2 * rank_dim, aux_width), amps, w_own, n_pair, n_aux, rank_dim
    )
    share_width = drive.shape[2]
    quarter = rank_dim // n_aux
    row_start = lax.axis_index("aux") * quarter
    keep_share = lax.dynamic_slice_in_dim(keep_rows, row_start, quarter, 1)
    coupled = sums[:, :quarter].reshape(local_pairs, quarter, 2, rank_dim)
    coupled = jnp.where(keep_share[:, :, None, None], coupled, 0.0).transpose(0, 2, 1, 3)
    occ_pair = jnp.sum(own_table * occ_energy[None, None, :], axis=(1, 2))
    energy_rows = lax.dynamic_slice_in_dim(pno_energy, row_start, quarter, 1)
    shift = energy_rows[:, :, None] + pno_energy[:, None, :] - occ_pair[:, None, None]
    signs = jnp.array([1.0, -1.0], jnp.float32)
    factor = shift[:, None] - signs[None, :, None, None] * frequency[0]
    amp_share = lax.dynamic_slice_in_dim(amplitudes, row_start, quarter, 2).astype(jnp.float32)
    rest = (factor * amp_share + coupled).reshape(local_pairs, 2, share_width)
    return drive + rest


def solution(mesh):
    placed = (
        P("pair", None, "aux"),
        P("pair", None, None, None),
        P("pair", None, "aux"),
        P("pair", None),
        P(),
        P(),
        P(),
        P("pair", None),
        P("pair"),
        P(),
    )
    return jax.shard_map(
        body, mesh=mesh, in_specs=placed, out_specs=P("pair", None, "aux"), check_vma=False
    )
```

profile of v0, /device:TPU:0, one launch (start us, length us, event | category | flops | bytes accessed | tf_op | source)
XLA Modules:
  0.0 67.3 jit_solution(8576467649835006478)
XLA Ops:
  0.0 0.0 copy-start
  0.0 0.0 copy-start.3
  0.0 0.0 copy-start.4
  0.0 0.7 %iota_compare_fusion = pred[2,120]{0,1:T(8,128)(4,1)S(1)} fusion(s32[2]{0:T(128)} %param.19), kind=kLoop, calls=%fused_computation.5 | loop fusion | flops 240 | bytes 248 | tf_op jit(solution)/shard_map/lt | solution.py:531
  0.7 0.1 copy.24
  0.8 1.0 %select_bitcast_fusion = bf16[2,120,2,120]{3,1,2,0:T(8,128)(2,1)S(1)} fusion(bf16[2,2,120,120]{3,2,1,0:T(8,128)(2,1)} %param.12, pred[2,120]{1,0:T(4,128)(4,1)S(1)} %copy.24), kind=kLoop, calls=%fused_computation.2 | loop fusion | flops 57600 | bytes 230640 | tf_op jit(solution)/shard_map/jit(_where)/select_n | solution.py:534
  1.8 0.1 copy.25
  1.9 0.0 copy-start.5
  1.9 0.0 copy-start.2
  2.0 0.0 copy-start.6
  2.0 0.1 reshape.47
  2.1 0.7 pad.10.a_ref
  2.7 0.7 %constant_dynamic-slice_fusion.2 = s32[2,2]{0,1:T(2,128)S(1)} fusion(s32[16,2]{0,1:T(2,128)} %param.17, s32[]{:T(128)S(6)} %select_n.20), kind=kLoop, calls=%fused_computation.21 | loop fusion | bytes 36 | tf_op jit(solution)/shard_map/dynamic_slice | solution.py:18
  3.5 0.1 copy.22
  3.6 0.0 copy-done
  3.6 0.0 copy-start.1
  3.6 0.2 fusion.1
  3.8 0.0 copy-done.3
  3.8 0.0 copy-done.4
  3.8 0.3 fusion
  4.1 0.1 select_reduce_fusion
  4.2 0.6 pad_convert_fusion.w_ref
  4.8 58.6 %shard_map.109 = f32[2,32,240]{2,1,0:T(8,128)} custom-call(bf16[240,2304]{1,0:T(8,128)(2,1)} %bitcast.19, bf16[256,240]{1,0:T(8,128)(2,1)} %pad.10.a_ref, f32[2,128]{1,0:T(2,128)} %pad_convert_fusion.w_ref), custom_call_target="tpu_custom_call" | custom-call | tf_op jit(solution)/shard_map/pallas_call | solution.py:460
  63.4 0.9 %reshape.53 = f32[2,30,2,120]{3,2,1,0:T(2,128)S(1)} reshape(f32[2,30,240]{2,1,0:T(8,128)} %bitcast.20) | data formatting | bytes 115200 | tf_op jit(solution)/shard_map/reshape | solution.py:545
  64.4 0.8 %constant_dynamic-slice_fusion.1 = bf16[2,2,30,120]{3,2,1,0:T(8,128)(2,1)S(1)} fusion(bf16[2,2,120,120]{3,2,1,0:T(8,128)(2,1)} %param.12, s32[]{:T(128)S(6)} %select_n.19), kind=kLoop, calls=%fused_computation.20 | loop fusion | bytes 57604 | tf_op jit(solution)/shard_map/dynamic_slice | solution.py:552
  65.2 0.0 copy-done.5
  65.2 0.2 select_reduce_fusion.1
  65.4 0.0 copy-done.2
  65.4 0.1 constant_dynamic-slice_fusion.3
  65.4 0.1 copy.21
  65.5 0.1 add_subtract_fusion
  66.3 0.0 copy-done.6
  66.3 0.1 bitcast_add_fusion
  66.5 0.1 reshape.49
  66.6 0.0 copy-done.1
  66.6 0.7 add.41
  (3 shorter events, 0.0 us)
Async XLA Ops:
  0.0 3.6 %copy-start = (f32[32,32]{1,0:T(8,128)S(1)}, f32[32,32]{1,0:T(8,128)}, u32[]{:S(2)}) copy-start(f32[32,32]{1,0:T(8,128)} %param.20) | copy-start | bytes 12292
  0.0 3.8 %copy-start.3 = (s32[16,2]{0,1:T(2,128)S(1)}, s32[16,2]{0,1:T(2,128)}, u32[]{:S(2)}) copy-start(s32[16,2]{0,1:T(2,128)} %param.17) | copy-start | bytes 388
  0.0 3.8 %copy-start.4 = (s32[2,8]{1,0:T(2,128)S(1)}, s32[2,8]{1,0:T(2,128)}, u32[]{:S(2)}) copy-start(s32[2,8]{1,0:T(2,128)} %param.18) | copy-start | bytes 196
  1.9 63.2 %copy-start.5 = (f32[32]{0:T(128)S(1)}, f32[32]{0:T(128)}, u32[]{:S(2)}) copy-start(f32[32]{0:T(128)} %param.15) | copy-start | bytes 388
  1.9 63.4 %copy-start.2 = (f32[2,120]{1,0:T(2,128)S(1)}, f32[2,120]{1,0:T(2,128)}, u32[]{:S(2)}) copy-start(f32[2,120]{1,0:T(2,128)} %param.14) | copy-start | bytes 2884
  2.0 64.3 %copy-start.6 = (f32[2]{0:T(128)S(1)}, f32[2]{0:T(128)}, u32[]{:S(2)}) copy-start(f32[2]{0:T(128)} %constant.29.clone) | copy-start | bytes 28
  3.6 63.0 %copy-start.1 = (f32[2,2,3600]{2,1,0:T(2,128)S(1)}, f32[2,2,3600]{2,1,0:T(2,128)}, u32[]{:S(2)}) copy-start(f32[2,2,3600]{2,1,0:T(2,128)} %param.13) | copy-start | bytes 172804
where the time goes:
time: 67.6 us; the launch traced here: 67.3 us
  Pallas kernels  58.6 us (87%)
  local copies, waits for them, and re-layouts  3.9 us (6%)
  other arithmetic  3.46 us (5%)
  between operations  0.79 us (1%)
    pallas_call x1, Pallas kernels, fused_coupling(): pl.pallas_call(functools.partial(kernel, n_pair, n_aux, rank), out_shape=...  58.6 us

commit v1 on v0

v1 whole, which is shorter than its diff:
```python
import functools

import jax
import jax.numpy as jnp
from jax import lax
from jax.experimental import pallas as pl
from jax.experimental.pallas import tpu as pltpu
from jax.sharding import PartitionSpec as P

LANE = 128


def pair_weights(pair_lmo, neighbours, fock_off, first_pair):
    local_pairs = neighbours.shape[0]
    total_pairs = pair_lmo.shape[0]
    lmo_count = fock_off.shape[0]
    lmo_ids = jnp.arange(lmo_count, dtype=jnp.int32)
    own_lmo = lax.dynamic_slice_in_dim(pair_lmo, first_pair, local_pairs, 0)
    own_table = (own_lmo[:, :, None] == lmo_ids[None, None, :]).astype(jnp.float32)
    lmo_table = (pair_lmo[:, :, None] == lmo_ids[None, None, :]).astype(jnp.float32)
    pair_ids = jnp.arange(total_pairs, dtype=jnp.int32)
    onehot = (neighbours[:, :, None] == pair_ids[None, None, :]).astype(jnp.float32)
    fock_rows = jnp.einsum("psl,lm->psm", own_table, fock_off, precision=lax.Precision.HIGHEST)
    near_table = jnp.einsum("pkn,nsl->pksl", onehot, lmo_table)
    values = jnp.sum(fock_rows[:, None, :, :] * near_table, axis=(2, 3))
    weights = jnp.sum(values[:, :, None] * onehot, axis=1).astype(jnp.bfloat16)
    return (weights, own_table)


def plain_body(
    panels,
    amplitudes,
    drive,
    pno_energy,
    occ_energy,
    frequency,
    pair_lmo,
    neighbours,
    pno_ranks,
    fock_off,
):
    local_pairs, rank_dim, aux_width = panels.shape
    total_pairs = pair_lmo.shape[0]
    n_pair = lax.axis_size("pair")
    n_aux = lax.axis_size("aux")
    first_pair = lax.axis_index("pair") * local_pairs
    rows_index = jnp.arange(rank_dim, dtype=jnp.int32)
    keep_rows = rows_index[None, :] < pno_ranks[:, None]
    weights, own_table = pair_weights(pair_lmo, neighbours, fock_off, first_pair)
    weights = lax.all_gather(weights, "pair", axis=0, tiled=True)
    amps = jnp.where(keep_rows[:, :, None, None], jnp.transpose(amplitudes, (0, 2, 1, 3)), 0)
    amps = lax.all_gather(
        amps.reshape(local_pairs * rank_dim, 2 * rank_dim), "pair", axis=0, tiled=True
    )
    masked = jnp.where(keep_rows[:, :, None], panels, jnp.zeros_like(panels))
    slices = lax.all_to_all(
        masked.reshape(local_pairs * rank_dim, aux_width), "pair", 1, 0, tiled=True
    )
    products = jnp.einsum("iq,jq->ij", slices, slices, preferred_element_type=jnp.float32)
    products = products.reshape(total_pairs, rank_dim, total_pairs, rank_dim)
    mixed = (products * weights.astype(jnp.float32)[:, None, :, None]).astype(jnp.bfloat16)
    mixed = mixed.reshape(total_pairs * rank_dim, total_pairs * rank_dim)
    coupled = jnp.dot(mixed, amps, preferred_element_type=jnp.float32).astype(jnp.bfloat16)
    share_width = drive.shape[2]
    coupled = coupled.reshape(total_pairs, rank_dim, 2, rank_dim).transpose(0, 2, 1, 3)
    coupled = coupled.reshape(n_pair, local_pairs, 2, n_aux, share_width).transpose(0, 3, 1, 2, 4)
    coupled = coupled.reshape(n_pair * n_aux, local_pairs, 2, share_width)
    coupled = lax.all_to_all(coupled, ("pair", "aux"), 0, 0, tiled=True)
    coupled_share = jnp.sum(coupled.astype(jnp.float32), axis=0)
    share_start = lax.axis_index("aux") * share_width
    occ_pair = jnp.sum(own_table * occ_energy[None, None, :], axis=(1, 2))
    shift = pno_energy[:, :, None] + pno_energy[:, None, :] - occ_pair[:, None, None]
    shift_flat = lax.dynamic_slice_in_dim(
        shift.reshape(local_pairs, rank_dim * rank_dim), share_start, share_width, 1
    )
    signs = jnp.array([1.0, -1.0], jnp.float32)
    factor = shift_flat[:, None, :] - signs[None, :, None] * frequency[0]
    amp_flat = amplitudes.reshape(local_pairs, 2, rank_dim * rank_dim)
    amp_share = lax.dynamic_slice_in_dim(amp_flat, share_start, share_width, 2).astype(jnp.float32)
    return drive + factor * amp_share + coupled_share


def remote(src, dst, send_sem, recv_sem, pair, aux):
    return pltpu.make_async_remote_copy(
        src_ref=src,
        dst_ref=dst,
        send_sem=send_sem,
        recv_sem=recv_sem,
        device_id=(pair, aux),
        device_id_type=pl.DeviceIdType.MESH,
    )


def kernel(
    n_pair, n_aux, rank, x_hbm, amp_hbm, energy_hbm, fock_hbm,
    occ_ref, frequency_ref, lmo_ref, neighbour_ref, rank_ref, out_ref,
    xv, amp_v, energy_v, fock_v, a_ref, term, xb, ab, wt, left_rows, acc, parts, parts_in, ends, ends_in,
    load_sem, small_sem, local_sem,
    x_send, x_recv, e_send, e_recv, f_send, f_recv, g_send, g_recv,
    a_send, a_recv, b_send, b_recv, p_send, p_recv, q_send, q_recv,
):
    me = lax.axis_index("pair")
    aux = lax.axis_index("aux")
    core = lax.rem(aux, 2)
    chip = aux // 2
    mate = aux + 1 - 2 * core
    n_chip = n_aux // 2
    block = 2 * rank
    tiles = xv.shape[1] // LANE
    base = (tiles // n_pair) * LANE
    extra = tiles % n_pair
    stride = n_pair // (2 * extra) if extra else 1
    share = a_ref.shape[0] // n_aux
    quarter = rank // n_aux
    padded = ends_in.shape[2]
    half = n_pair // 2
    near = (me // half) * half
    far = half - near
    spot_me = me - near
    across = far + spot_me

    loads = load_sem.shape[0]
    piece = xv.shape[1] // loads

    def load_x(s):
        lanes = pl.ds(s * piece, piece)
        return pltpu.make_async_copy(x_hbm.at[:, lanes], xv.at[:, lanes], load_sem.at[s])

    smalls = [
        pltpu.make_async_copy(amp_hbm, amp_v, small_sem.at[0]),
        pltpu.make_async_copy(fock_hbm, fock_v, small_sem.at[1]),
        pltpu.make_async_copy(energy_hbm, energy_v, small_sem.at[2]),
    ]
    for copy in smalls:
        copy.start()
    for s in range(loads):
        load_x(s).start()

    barrier = pltpu.get_barrier_semaphore()

    def greet(pair, other):
        pl.semaphore_signal(
            barrier, inc=1, device_id=(pair, other), device_id_type=pl.DeviceIdType.MESH
        )

    def near_peer(t):
        return near + lax.rem(spot_me + t, half)

    def far_peer(t):
        return far + lax.rem(spot_me + t, half)

    def row(u):
        return 2 * lax.rem(chip + u, n_chip) + core

    for t in range(half):
        greet(far_peer(t), aux)
    for t in range(1, half):
        greet(near_peer(t), aux)
        for u in range(1, n_chip):
            greet(near_peer(t), row(u))
    greet(across, mate)
    for t in range(1, n_aux):
        greet(me, lax.rem(aux + t, n_aux))

    def holder(which, level):
        spot = 2 * level + which
        shift = spot % 2 if not hasattr(spot, "dtype") else lax.rem(spot, 2)
        return stride * spot + (shift if stride > 1 else 0)

    lanes = pl.ds(pl.multiple_of(core * base, LANE), base)
    mate_lanes = pl.ds(pl.multiple_of((1 - core) * base, LANE), base)
    extra_lanes = pl.ds(2 * base, LANE)
    my_share = pl.ds(pl.multiple_of(aux * share, 16), share)

    def own_cols(peer):
        return xv.at[:, pl.ds(pl.multiple_of(peer * base, LANE), base)]

    def send_a(t):
        peer = near_peer(t) if t else across
        return remote(a_ref.at[my_share], ab.at[me, my_share], a_send.at[t], a_recv.at[me], peer, aux)

    def pass_a(t):
        rows = ab.at[across, my_share]
        return remote(rows, rows, a_send.at[half + t], a_recv.at[across], near_peer(t), aux)

    def wait_a(j):
        remote(
            a_ref.at[my_share], ab.at[j, my_share], a_send.at[0], a_recv.at[j], me, mate
        ).wait_recv()

    def send_x(peer):
        return remote(
            own_cols(peer), xb.at[me, :, lanes], x_send.at[peer], x_recv.at[me], peer, aux
        )

    def wait_x(j):
        remote(
            own_cols(me), xb.at[j, :, lanes], x_send.at[j], x_recv.at[j], me, mate
        ).wait_recv()

    def wait_f(j):
        remote(
            own_cols(me), xb.at[j, :, mate_lanes], f_send.at[j], f_recv.at[j], me, mate
        ).wait_recv()

    def extra_cols(level):
        return xv.at[:, pl.ds(base * n_pair + level * LANE, LANE)]

    def send_e(level):
        return remote(
            extra_cols(level), xb.at[me, :, extra_lanes], e_send.at[level], e_recv.at[me],
            holder(core, level), aux,
        )

    def send_f(j):
        return remote(xb.at[j, :, lanes], xb.at[j, :, lanes], f_send.at[j], f_recv.at[j], me, mate)

    def own_f():
        return remote(own_cols(me), xb.at[me, :, lanes], f_send.at[me], f_recv.at[me], me, mate)

    def send_g(j):
        return remote(
            xb.at[j, :, extra_lanes], xb.at[j, :, extra_lanes], g_send.at[j], g_recv.at[j], me, mate
        )

    def send_b(j, u):
        rows = ab.at[j, my_share]
        return remote(rows, rows, b_send.at[j, u], b_recv.at[aux, j], me, lax.rem(aux + u, n_aux))

    mine_x = pltpu.make_async_copy(own_cols(me), xb.at[me, :, lanes], local_sem.at[0])
    mine_a = pltpu.make_async_copy(a_ref, ab.at[me], local_sem.at[1])

    def holds(which):
        found = me < 0
        for level in range(extra):
            found = jnp.logical_or(found, holder(which, level) == me)
        return found

    self_holds = holds(core)
    mate_holds = holds(1 - core)
    if extra:
        @pl.when(jnp.logical_not(jnp.logical_or(self_holds, mate_holds)))
        def _():
            xb[:, :, 2 * base :] = jnp.zeros((n_pair, block, LANE), xb.dtype)

    for copy in smalls:
        copy.wait()
    own_amplitudes(rank, me, amp_v, fock_v, lmo_ref, neighbour_ref, rank_ref, a_ref)
    mine_a.start()
    for s in range(loads):
        load_x(s).wait()
    pl.semaphore_wait(barrier, n_pair + (half - 1) * (n_chip - 1) + n_aux - 1)

    for t in range(half):
        send_a(t).start()
    for level in range(extra):
        @pl.when(holder(core, level) != me)
        def _():
            send_e(level).start()

        @pl.when(holder(core, level) == me)
        def _():
            pltpu.make_async_copy(
                extra_cols(level), xb.at[me, :, extra_lanes], local_sem.at[2]
            ).start()
    level = me // (half // 2)
    inner = jnp.logical_or(level == 1, level == 2)

    @pl.when(inner)
    def _():
        for t in range(half):
            send_x(far_peer(t)).start()

    own_f().start()
    mine_x.start()
    own_term(rank, n_aux, me, aux, amp_v, energy_v, occ_ref, frequency_ref, lmo_ref, term)

    wait_a(across)
    for t in range(1, half):
        pass_a(t).start()
    for u in range(1, n_aux):
        send_b(across, u).start()
    for t in range(1, half):
        send_x(near_peer(t)).start()

    @pl.when(jnp.logical_not(inner))
    def _():
        for t in range(half):
            send_x(far_peer(t)).start()

    for t in range(1, half):
        j = near_peer(half - t)
        wait_a(j)
        for u in range(1, n_aux):
            send_b(j, u).start()
    for t in range(1, half):
        j = far_peer(half - t)
        wait_a(j)
        for u in range(1, n_aux):
            send_b(j, u).start()
    mine_x.wait()
    mine_a.wait()
    if extra:
        @pl.when(self_holds)
        def _():
            pltpu.make_async_copy(
                extra_cols(0), xb.at[me, :, extra_lanes], local_sem.at[2]
            ).wait()
            send_g(me).start()
            for t in range(1, n_pair):
                j = lax.rem(me + n_pair - t, n_pair)
                remote(
                    extra_cols(0), xb.at[j, :, extra_lanes], e_send.at[0], e_recv.at[j], me, mate
                ).wait_recv()
                send_g(j).start()

        @pl.when(mate_holds)
        def _():
            for j in range(n_pair):
                send_g(j).wait_recv()
    for t in range(1, half):
        j = near_peer(half - t)
        wait_x(j)
        send_f(j).start()
    for t in range(1, n_pair):
        j = lax.rem(me + n_pair - t, n_pair)
        for u in range(1, n_aux):
            other = lax.rem(aux + u, n_aux)
            rows = ab.at[j, pl.ds(pl.multiple_of(other * share, 16), share)]
            remote(rows, rows, b_send.at[j, u], b_recv.at[other, j], me, other).wait_recv()

    rows = [ab[j, block : block + 16, :LANE].astype(jnp.float32) for j in range(n_pair)]
    rows = [jnp.where(core == 0, r[0:1], r[1:2]) for r in rows]
    table = jnp.concatenate(rows, axis=0).astype(jnp.bfloat16)
    pair_row = lax.broadcasted_iota(jnp.int32, (LANE, block), 0)
    column = lax.broadcasted_iota(jnp.int32, (LANE, block), 1)
    for j in range(n_pair):
        pick = pair_row == jnp.where(column < rank, 2 * j, 2 * j + 1)
        pick = jnp.where(pick, 1.0, 0.0).astype(jnp.bfloat16)
        wt[j] = jnp.dot(table, pick, preferred_element_type=jnp.float32)

    def collect_rows(i):
        for side in range(2):
            @pl.when(core == side)
            def _():
                left_rows[i] = xb[i, side * rank : (side + 1) * rank, :]

    def join(pieces):
        return jnp.concatenate(pieces, axis=0) if len(pieces) > 1 else pieces[0]

    def turned(indices, blocks):
        rows = join([left_rows[i] for i in indices])
        columns = join([xb[j] for j in blocks])
        products = lax.dot_general(
            rows, columns, (((1,), (1,)), ((), ())), preferred_element_type=jnp.float32
        )
        total = None
        for m, j in enumerate(blocks):
            part = products[:, m * block : (m + 1) * block]
            scaled = [
                part[k * rank : (k + 1) * rank] * wt[j, pl.ds(i, 1), :]
                for k, i in enumerate(indices)
            ]
            turn = jnp.dot(
                join(scaled).astype(jnp.bfloat16), ab[j, :block, :],
                preferred_element_type=jnp.float32,
            )
            total = turn if total is None else total + turn
        return total

    def couple(indices, blocks, first=False):
        turn = turned(indices, blocks)
        for k, i in enumerate(indices):
            rows = turn[k * rank : (k + 1) * rank]
            if first:
                acc[i, :rank, :] = rows
            else:
                acc[i, :rank, :] += rows

    near_all = [near + t for t in range(half)]
    for t in range(half):
        wait_f(near_peer(t))
        collect_rows(near_peer(t))
    for t in range(half):
        couple(near_all, [near + t], first=t == 0)

    def send_p(which, t, u):
        peer = near_peer(t)
        other = lax.rem(chip + u, n_chip)
        i = far_peer(t) if which else peer
        return remote(
            parts.at[i, other], parts_in.at[which, t, u], p_send.at[which, t, u],
            p_recv.at[which, t, u], peer, 2 * other + core,
        )

    hops = [(t, u) for t in range(half) for u in range(n_chip) if t or u]

    def spread(which):
        for t in range(half):
            i = far_peer(t) if which else near_peer(t)
            for k in range(n_aux):
                rows = acc[i, quarter * k : quarter * k + padded, :]
                parts[i, k // 2, (k % 2) * padded : (k % 2 + 1) * padded, :] = rows.astype(
                    parts.dtype
                )
            for u in range(n_chip):
                if t or u:
                    send_p(which, t, u).start()

    for k in range(half):
        e = far_peer((half - k) % half)
        earlier = [far_peer((half - m) % half) for m in range(k)]
        wait_x(e)
        send_f(e).start()
        wait_f(e)
        collect_rows(e)

        couple([e], near_all + earlier + [e], first=True)
        if earlier:
            couple(earlier, [e])
        if k == half - 1:
            spread(1)
        couple(near_all, [e])
    spread(0)

    def collect(which):
        i = across if which else me
        total = parts[i, chip].astype(jnp.float32)
        for t, u in hops:
            send_p(which, t, u).wait_recv()
            total = total + parts_in[which, t, u].astype(jnp.float32)
        ends[which] = total.astype(ends.dtype)

    def send_q(k):
        return remote(
            ends.at[1, pl.ds(k * padded, padded)], ends_in.at[1, core],
            q_send.at[k], q_recv.at[1, core], across, 2 * chip + k,
        )

    def mate_q():
        return remote(
            ends.at[0, pl.ds(pl.multiple_of((1 - core) * padded, padded), padded)],
            ends_in.at[0, core], q_send.at[2], q_recv.at[0, core], me, mate,
        )

    collect(1)
    for k in range(2):
        send_q(k).start()
    collect(0)
    mate_q().start()
    ends_in[0, core] = ends[0, pl.ds(pl.multiple_of(core * padded, padded), padded), :]

    def arrive(which, side):
        remote(
            ends.at[which, pl.ds(0, padded)], ends_in.at[which, side],
            q_send.at[0], q_recv.at[which, side], me, mate,
        ).wait_recv()

    arrive(0, 1 - core)
    for side in range(2):
        arrive(1, side)
        total = ends_in[0, side].astype(jnp.float32) + ends_in[1, side].astype(jnp.float32)
        at = lax.broadcasted_iota(jnp.int32, (padded, LANE), 0) + aux * quarter
        for s in range(2):
            part = total[:, s * LANE : (s + 1) * LANE]
            part = jnp.where(at < rank_ref[side], part, 0.0)
            part = part + term[side, s, pl.ds(aux * quarter, padded), :]
            for r in range(quarter):
                out_ref[side, s : s + 1, r * rank : (r + 1) * rank] = part[r : r + 1, :rank]

    for t in range(half):
        send_a(t).wait_send()
        send_x(far_peer(t)).wait_send()
        if t:
            pass_a(t).wait_send()
            send_x(near_peer(t)).wait_send()
    for t in range(1, n_pair):
        j = lax.rem(me + n_pair - t, n_pair)
        send_f(j).wait_send()
        for u in range(1, n_aux):
            send_b(j, u).wait_send()
    own_f().wait_send()
    for level in range(extra):
        @pl.when(holder(core, level) != me)
        def _():
            send_e(level).wait_send()
    if extra:
        @pl.when(self_holds)
        def _():
            for j in range(n_pair):
                send_g(j).wait_send()
    for which in range(2):
        for t, u in hops:
            send_p(which, t, u).wait_send()
    for k in range(2):
        send_q(k).wait_send()
    mate_q().wait_send()


def own_amplitudes(rank, me, amp_v, fock_v, lmo_ref, neighbour_ref, rank_ref, a_ref):
    total_pairs = lmo_ref.shape[1]
    lmo_count = fock_v.shape[0]
    a_ref[...] = jnp.zeros_like(a_ref)
    at = lax.broadcasted_iota(jnp.int32, (rank, rank), 0)
    for p in range(2):
        for s in range(2):
            part = jnp.where(at < rank_ref[p], amp_v[p, s].astype(jnp.float32), 0.0)
            a_ref[p * rank : (p + 1) * rank, s * LANE : s * LANE + rank] = part.astype(a_ref.dtype)
    lane = lax.broadcasted_iota(jnp.int32, (1, LANE), 1)
    level = lax.broadcasted_iota(jnp.int32, (lmo_count, LANE), 0)
    values = 0.0
    for side in range(2):
        where = jnp.full((1, LANE), -1, jnp.int32)
        for n in range(total_pairs):
            where = jnp.where(lane == n, lmo_ref[side, n], where)
        table = jnp.where(level == where, 1.0, 0.0)
        rows = [fock_v[pl.ds(lmo_ref[side, 2 * me + p], 1), :] for p in range(2)]
        rows = jnp.concatenate(rows + [jnp.zeros((6, lmo_count), jnp.float32)], axis=0)
        values = values + jnp.dot(
            rows, table, preferred_element_type=jnp.float32, precision=lax.Precision.HIGHEST
        )
    counts = []
    for p in range(2):
        count = jnp.zeros((1, LANE), jnp.float32)
        for k in range(neighbour_ref.shape[1]):
            count = count + jnp.where(lane == neighbour_ref[p, k], 1.0, 0.0)
        counts.append(count)
    counts = jnp.concatenate(counts + [jnp.zeros((6, LANE), jnp.float32)], axis=0)
    rows = jnp.concatenate([values * counts, jnp.zeros((8, LANE), jnp.float32)], axis=0)
    a_ref[2 * rank : 2 * rank + 16, :LANE] = rows.astype(a_ref.dtype)


def own_term(rank, n_aux, me, aux, amp_v, energy_v, occ_ref, frequency_ref, lmo_ref, term):
    row = lax.broadcasted_iota(jnp.int32, (rank, rank), 0)
    column = lax.broadcasted_iota(jnp.int32, (rank, rank), 1)
    term[...] = jnp.zeros_like(term)
    for p in range(2):
        energy = jnp.broadcast_to(energy_v[p : p + 1, :], (rank, rank))
        own = jnp.sum(jnp.where(row == column, energy, 0.0), axis=1, keepdims=True)
        pair = 2 * me + p
        occ = occ_ref[lmo_ref[0, pair]] + occ_ref[lmo_ref[1, pair]]
        shift = own + energy - occ
        for s in range(2):
            factor = shift - frequency_ref[0] if s == 0 else shift + frequency_ref[0]
            term[p, s, :rank, :rank] = factor * amp_v[p, s].astype(jnp.float32)


def fused_coupling(
    x_own, amplitudes, energy, fock, occ, frequency, lmo, neighbours, ranks, n_pair, n_aux, rank
):
    block = 2 * rank
    tiles = x_own.shape[1] // LANE
    depth = 2 * (tiles // n_pair) * LANE + (LANE if tiles % n_pair else 0)
    n_chip = n_aux // 2
    half = n_pair // 2
    extra = max(tiles % n_pair, 1)
    wide = 2 * LANE
    a_shape = (-(-(block + 16) // (16 * n_aux)) * 16 * n_aux, wide)
    padded = -(-(rank // n_aux) // 16) * 16
    tall = -(-(rank - rank // n_aux + padded) // 8) * 8
    loads = 2 if tiles % 2 == 0 else 1
    dma = pltpu.SemaphoreType.DMA
    bf16 = jnp.bfloat16
    anywhere = pl.BlockSpec(memory_space=pl.ANY)
    scalars = pl.BlockSpec(memory_space=pltpu.SMEM)
    return pl.pallas_call(
        functools.partial(kernel, n_pair, n_aux, rank),
        out_shape=jax.ShapeDtypeStruct((2, 2, rank // n_aux * rank), jnp.float32),
        in_specs=[anywhere] * 4 + [scalars] * 5,
        out_specs=pl.BlockSpec(memory_space=pltpu.VMEM),
        scratch_shapes=[
            pltpu.VMEM(x_own.shape, bf16),
            pltpu.VMEM(amplitudes.shape, bf16),
            pltpu.VMEM(energy.shape, jnp.float32),
            pltpu.VMEM(fock.shape, jnp.float32),
            pltpu.VMEM(a_shape, bf16),
            pltpu.VMEM((2, 2, tall, LANE), jnp.float32),
            pltpu.VMEM((n_pair, block, depth), bf16),
            pltpu.VMEM((n_pair,) + a_shape, bf16),
            pltpu.VMEM((n_pair, n_pair, block), jnp.float32),
            pltpu.VMEM((n_pair, rank, depth), bf16),
            pltpu.VMEM((n_pair, tall, wide), jnp.float32),
            pltpu.VMEM((n_pair, n_chip, 2 * padded, wide), bf16),
            pltpu.VMEM((2, half, n_chip, 2 * padded, wide), bf16),
            pltpu.VMEM((2, 2 * padded, wide), bf16),
            pltpu.VMEM((2, 2, padded, wide), bf16),
            dma((loads,)), dma((3,)), dma((3,)),
            dma((n_pair,)), dma((n_pair,)),
            dma((extra,)), dma((n_pair,)),
            dma((n_pair,)), dma((n_pair,)),
            dma((n_pair,)), dma((n_pair,)),
            dma((n_pair,)), dma((n_pair,)),
            dma((n_pair, n_aux)), dma((n_aux, n_pair)),
            dma((2, half, n_chip)), dma((2, half, n_chip)),
            dma((3,)), dma((2, 2)),
        ],
        compiler_params=pltpu.CompilerParams(collective_id=0, has_side_effects=True),
    )(x_own, amplitudes, energy, fock, occ, frequency, lmo, neighbours, ranks)


def fits(panels, n_pair, n_aux):
    local_pairs, rank, width = panels.shape
    tiles = width // LANE
    extra = tiles % n_pair
    return (
        local_pairs == 2
        and width % LANE == 0
        and rank % 8 == 0
        and rank % n_aux == 0
        and n_aux % 2 == 0
        and n_pair % 2 == 0
        and 2 * n_pair <= LANE
        and tiles >= n_pair
        and (extra == 0 or n_pair % (2 * extra) == 0)
    )


def body(*operands):
    if fits(operands[0], lax.axis_size("pair"), lax.axis_size("aux")):
        return kernel_body(*operands)
    return plain_body(*operands)


def kernel_body(
    panels,
    amplitudes,
    drive,
    pno_energy,
    occ_energy,
    frequency,
    pair_lmo,
    neighbours,
    pno_ranks,
    fock_off,
):
    local_pairs, rank_dim, aux_width = panels.shape
    coupled = fused_coupling(
        panels.reshape(2 * rank_dim, aux_width), amplitudes, pno_energy, fock_off, occ_energy,
        frequency, pair_lmo.T, neighbours, pno_ranks,
        lax.axis_size("pair"), lax.axis_size("aux"), rank_dim,
    )
    return drive + coupled


def solution(mesh):
    placed = (
        P("pair", None, "aux"),
        P("pair", None, None, None),
        P("pair", None, "aux"),
        P("pair", None),
        P(),
        P(),
        P(),
        P("pair", None),
        P("pair"),
        P(),
    )
    return jax.shard_map(
        body, mesh=mesh, in_specs=placed, out_specs=P("pair", None, "aux"), check_vma=False
    )
```

time: 67.6 us -> 51.3 us (0.76)
  Pallas kernels: 58.6 us -> 48.9 us
  local copies, waits for them, and re-layouts: 3.9 us -> 0.01 us
  other arithmetic: 3.46 us -> 1.48 us
    pallas_call x1, Pallas kernels: 58.6 us -> 48.9 us  [fused_coupling(): pl.pallas_call(functools.partial(kernel, n_pair, n_aux, rank), out_shape=...]
    dynamic_slice x6 -> x0, local copies, waits for them, and re-layouts: 1.84 us -> none  [the longest x2 0.84 us: pair_weights(): own_lmo = lax.dynamic_slice_in_dim(pair_lmo, first_pair, local_pairs, 0)]
    reshape x3 -> x0, local copies, waits for them, and re-layouts: 1.18 us -> none  [the longest x1 0.94 us: kernel_body(): coupled = sums[:, :quarter].reshape(local_pairs, quarter, 2, rank_dim)]
    select_n x1 -> x0, other arithmetic: 1.02 us -> none  [kernel_body(): jnp.where(keep_rows[:, :, None, None], jnp.transpose(amplitudes, (0, 2, 1...]
    lt x1 -> x0, other arithmetic: 0.71 us -> none  [kernel_body(): keep_rows = rows_index[None, :] < pno_ranks[:, None]]
    add x2 -> x1, other arithmetic: 0.79 us -> 1.48 us  [kernel_body(): return drive + coupled]
where the time goes in v1:
time: 51.3 us; the launch traced here: 51.1 us
  Pallas kernels  48.9 us (95%)
  other arithmetic  1.48 us (3%)
  between operations  0.68 us (1%)
    pallas_call x1, Pallas kernels, fused_coupling(): pl.pallas_call(functools.partial(kernel, n_pair, n_aux, rank), out_shape=...  48.9 us
    add x1, other arithmetic, kernel_body(): return drive + coupled  1.48 us

profile of v1, /device:TPU:0, one launch (start us, length us, event | category | flops | bytes accessed | tf_op | source)
XLA Modules:
  0.0 51.1 jit_solution(6476856631277687837)
XLA Ops:
  0.0 0.0 copy-start
  0.7 48.9 %shard_map.100 = f32[2,2,3600]{2,1,0:T(2,128)} custom-call(bf16[240,2304]{1,0:T(8,128)(2,1)} %bitcast.2, bf16[2,2,120,120]{3,2,1,0:T(8,128)(2,1)} %amp_hbm.1, f32[2,120]{1,0:T(2,128)} %energy_hbm.1, f32[32,32]{1,0:T(8,128)} %fock_hbm.1, f32[32]{0:T(128)} %occ_ref.1, f32[1]{0:T(128)S(6)} %copy.11.frequency_ref, s32[2,16]{1,0:T(2,128)} %bitcast.3, ...), custom_call_target="tpu_custom_call" | custom-call | tf_op jit(solution)/shard_map/pallas_call | solution.py:566
  49.6 0.0 copy-done
  49.6 1.5 %add.3 = f32[2,2,3600]{2,1,0:T(2,128)} add(f32[2,2,3600]{2,1,0:T(2,128)S(1)} %copy-done, f32[2,2,3600]{2,1,0:T(2,128)} %shard_map.100) | non-fusion elementwise | flops 14400 | bytes 172800 | tf_op jit(solution)/shard_map/add | solution.py:642
Async XLA Ops:
  0.0 49.6 %copy-start = (f32[2,2,3600]{2,1,0:T(2,128)S(1)}, f32[2,2,3600]{2,1,0:T(2,128)}, u32[]{:S(2)}) copy-start(f32[2,2,3600]{2,1,0:T(2,128)} %param.12) | copy-start | bytes 172804

commit v2 on v1

--- a/solution.py
+++ b/solution.py
@@ -93,8 +93,9 @@
 
 def kernel(
     n_pair, n_aux, rank, x_hbm, amp_hbm, energy_hbm, fock_hbm,
-    occ_ref, frequency_ref, lmo_ref, neighbour_ref, rank_ref, out_ref,
-    xv, amp_v, energy_v, fock_v, a_ref, term, xb, ab, wt, left_rows, acc, parts, parts_in, ends, ends_in,
+    occ_hbm, frequency_hbm, lmo_hbm, neighbour_hbm, rank_hbm, out_ref,
+    xv, amp_v, energy_v, fock_v, occ_ref, frequency_ref, lmo_ref, neighbour_ref, rank_ref,
+    a_ref, term, xb, ab, wt, products, turned_products, left_rows, acc, parts, parts_in, ends, ends_in, nears,
     load_sem, small_sem, local_sem,
     x_send, x_recv, e_send, e_recv, f_send, f_recv, g_send, g_recv,
     a_send, a_recv, b_send, b_recv, p_send, p_recv, q_send, q_recv,
@@ -109,10 +110,9 @@
     tiles = xv.shape[1] // LANE
     base = (tiles // n_pair) * LANE
     extra = tiles % n_pair
-    stride = n_pair // (2 * extra) if extra else 1
     share = a_ref.shape[0] // n_aux
     quarter = rank // n_aux
-    padded = ends_in.shape[2]
+    padded = ends.shape[1]
     half = n_pair // 2
     near = (me // half) * half
     far = half - near
@@ -127,9 +127,12 @@
         return pltpu.make_async_copy(x_hbm.at[:, lanes], xv.at[:, lanes], load_sem.at[s])
 
     smalls = [
-        pltpu.make_async_copy(amp_hbm, amp_v, small_sem.at[0]),
-        pltpu.make_async_copy(fock_hbm, fock_v, small_sem.at[1]),
-        pltpu.make_async_copy(energy_hbm, energy_v, small_sem.at[2]),
+        pltpu.make_async_copy(source, target, small_sem.at[s])
+        for s, (source, target) in enumerate([
+            (amp_hbm, amp_v), (fock_hbm, fock_v), (energy_hbm, energy_v), (occ_hbm, occ_ref),
+            (frequency_hbm, frequency_ref), (lmo_hbm, lmo_ref), (neighbour_hbm, neighbour_ref),
+            (rank_hbm, rank_ref),
+        ])
     ]
     for copy in smalls:
         copy.start()
@@ -156,76 +159,82 @@
         greet(far_peer(t), aux)
     for t in range(1, half):
         greet(near_peer(t), aux)
-        for u in range(1, n_chip):
-            greet(near_peer(t), row(u))
-    greet(across, mate)
+        for v in range(1, n_aux):
+            greet(near_peer(t), lax.rem(aux + v, n_aux))
     for t in range(1, n_aux):
         greet(me, lax.rem(aux + t, n_aux))
 
     def holder(which, level):
-        spot = 2 * level + which
-        shift = spot % 2 if not hasattr(spot, "dtype") else lax.rem(spot, 2)
-        return stride * spot + (shift if stride > 1 else 0)
-
-    lanes = pl.ds(pl.multiple_of(core * base, LANE), base)
-    mate_lanes = pl.ds(pl.multiple_of((1 - core) * base, LANE), base)
-    extra_lanes = pl.ds(2 * base, LANE)
+        return half // 2 * (1 + level) + which
+
+    first = base + (LANE if extra else 0)
+    lanes = pl.ds(0, base)
+    mate_lanes = pl.ds(first, base)
+    extra_lanes = pl.ds(base, LANE)
     my_share = pl.ds(pl.multiple_of(aux * share, 16), share)
 
     def own_cols(peer):
         return xv.at[:, pl.ds(pl.multiple_of(peer * base, LANE), base)]
 
+    def await_bytes(view, send, recv):
+        return remote(view, view, send, recv, me, mate)
+
     def send_a(t):
         peer = near_peer(t) if t else across
-        return remote(a_ref.at[my_share], ab.at[me, my_share], a_send.at[t], a_recv.at[me], peer, aux)
+        return remote(
+            a_ref.at[my_share], ab.at[me, my_share], a_send.at[0], a_recv.at[1 if t else 0], peer, aux
+        )
 
     def pass_a(t):
         rows = ab.at[across, my_share]
-        return remote(rows, rows, a_send.at[half + t], a_recv.at[across], near_peer(t), aux)
-
-    def wait_a(j):
-        remote(
-            a_ref.at[my_share], ab.at[j, my_share], a_send.at[0], a_recv.at[j], me, mate
-        ).wait_recv()
+        return remote(rows, rows, a_send.at[0], a_recv.at[2], near_peer(t), aux)
+
+    def shares(blocks, count):
+        return ab.at[pl.ds(0, blocks), pl.ds(0, count * share)]
+
+    def wait_a(which):
+        blocks = half - 1 if which else 1
+        await_bytes(shares(blocks, 1), a_send.at[0], a_recv.at[which]).wait_recv()
 
     def send_x(peer):
         return remote(
-            own_cols(peer), xb.at[me, :, lanes], x_send.at[peer], x_recv.at[me], peer, aux
+            own_cols(peer), xb.at[me, :, lanes], x_send.at[0], x_recv.at[me], peer, aux
         )
 
     def wait_x(j):
-        remote(
-            own_cols(me), xb.at[j, :, lanes], x_send.at[j], x_recv.at[j], me, mate
-        ).wait_recv()
-
-    def wait_f(j):
-        remote(
-            own_cols(me), xb.at[j, :, mate_lanes], f_send.at[j], f_recv.at[j], me, mate
-        ).wait_recv()
+        await_bytes(xb.at[j, :, lanes], x_send.at[0], x_recv.at[j]).wait_recv()
+
+    def wait_f(k):
+        await_bytes(xb.at[0, :, mate_lanes], f_send.at[0], f_recv.at[k]).wait_recv()
 
     def extra_cols(level):
         return xv.at[:, pl.ds(base * n_pair + level * LANE, LANE)]
 
     def send_e(level):
         return remote(
-            extra_cols(level), xb.at[me, :, extra_lanes], e_send.at[level], e_recv.at[me],
+            extra_cols(level), xb.at[me, :, extra_lanes], e_send.at[level], e_recv.at[0],
             holder(core, level), aux,
         )
 
-    def send_f(j):
-        return remote(xb.at[j, :, lanes], xb.at[j, :, lanes], f_send.at[j], f_recv.at[j], me, mate)
+    def send_f(j, k):
+        return remote(
+            xb.at[j, :, lanes], xb.at[j, :, mate_lanes], f_send.at[0], f_recv.at[k], me, mate
+        )
 
     def own_f():
-        return remote(own_cols(me), xb.at[me, :, lanes], f_send.at[me], f_recv.at[me], me, mate)
-
-    def send_g(j):
         return remote(
-            xb.at[j, :, extra_lanes], xb.at[j, :, extra_lanes], g_send.at[j], g_recv.at[j], me, mate
-        )
-
-    def send_b(j, u):
+            own_cols(me), xb.at[me, :, mate_lanes], f_send.at[0], f_recv.at[half], me, mate
+        )
+
+    def send_g():
+        view = xb.at[:, :, extra_lanes]
+        return remote(view, view, g_send.at[0], g_recv.at[0], me, mate)
+
+    def send_b(j, u, which):
         rows = ab.at[j, my_share]
-        return remote(rows, rows, b_send.at[j, u], b_recv.at[aux, j], me, lax.rem(aux + u, n_aux))
+        return remote(
+            rows, rows, b_send.at[0], b_recv.at[which], me, lax.rem(aux + u, n_aux)
+        )
 
     mine_x = pltpu.make_async_copy(own_cols(me), xb.at[me, :, lanes], local_sem.at[0])
     mine_a = pltpu.make_async_copy(a_ref, ab.at[me], local_sem.at[1])
@@ -241,7 +250,7 @@
     if extra:
         @pl.when(jnp.logical_not(jnp.logical_or(self_holds, mate_holds)))
         def _():
-            xb[:, :, 2 * base :] = jnp.zeros((n_pair, block, LANE), xb.dtype)
+            xb[:, :, base:first] = jnp.zeros((n_pair, block, LANE), xb.dtype)
 
     for copy in smalls:
         copy.wait()
@@ -249,7 +258,7 @@
     mine_a.start()
     for s in range(loads):
         load_x(s).wait()
-    pl.semaphore_wait(barrier, n_pair + (half - 1) * (n_chip - 1) + n_aux - 1)
+    pl.semaphore_wait(barrier, half + half * n_aux - 1)
 
     for t in range(half):
         send_a(t).start()
@@ -263,6 +272,7 @@
             pltpu.make_async_copy(
                 extra_cols(level), xb.at[me, :, extra_lanes], local_sem.at[2]
             ).start()
+    send_x(near_peer(half // 2)).start()
     level = me // (half // 2)
     inner = jnp.logical_or(level == 1, level == 2)
 
@@ -275,29 +285,28 @@
     mine_x.start()
     own_term(rank, n_aux, me, aux, amp_v, energy_v, occ_ref, frequency_ref, lmo_ref, term)
 
-    wait_a(across)
+    wait_a(0)
     for t in range(1, half):
         pass_a(t).start()
     for u in range(1, n_aux):
-        send_b(across, u).start()
+        send_b(across, u, 1).start()
     for t in range(1, half):
-        send_x(near_peer(t)).start()
+        if t != half // 2:
+            send_x(near_peer(t)).start()
 
     @pl.when(jnp.logical_not(inner))
     def _():
         for t in range(half):
             send_x(far_peer(t)).start()
 
+    wait_a(1)
     for t in range(1, half):
-        j = near_peer(half - t)
-        wait_a(j)
         for u in range(1, n_aux):
-            send_b(j, u).start()
+            send_b(near_peer(t), u, 0).start()
+    wait_a(2)
     for t in range(1, half):
-        j = far_peer(half - t)
-        wait_a(j)
         for u in range(1, n_aux):
-            send_b(j, u).start()
+            send_b(far_peer(t), u, 1).start()
     mine_x.wait()
     mine_a.wait()
     if extra:
@@ -306,60 +315,65 @@
             pltpu.make_async_copy(
                 extra_cols(0), xb.at[me, :, extra_lanes], local_sem.at[2]
             ).wait()
-            send_g(me).start()
-            for t in range(1, n_pair):
-                j = lax.rem(me + n_pair - t, n_pair)
-                remote(
-                    extra_cols(0), xb.at[j, :, extra_lanes], e_send.at[0], e_recv.at[j], me, mate
-                ).wait_recv()
-                send_g(j).start()
+            await_bytes(
+                xb.at[pl.ds(0, n_pair - 1), :, extra_lanes], e_send.at[0], e_recv.at[0]
+            ).wait_recv()
+            send_g().start()
 
         @pl.when(mate_holds)
         def _():
-            for j in range(n_pair):
-                send_g(j).wait_recv()
+            send_g().wait_recv()
     for t in range(1, half):
         j = near_peer(half - t)
         wait_x(j)
-        send_f(j).start()
-    for t in range(1, n_pair):
-        j = lax.rem(me + n_pair - t, n_pair)
-        for u in range(1, n_aux):
-            other = lax.rem(aux + u, n_aux)
-            rows = ab.at[j, pl.ds(pl.multiple_of(other * share, 16), share)]
-            remote(rows, rows, b_send.at[j, u], b_recv.at[other, j], me, other).wait_recv()
-
-    rows = [ab[j, block : block + 16, :LANE].astype(jnp.float32) for j in range(n_pair)]
-    rows = [jnp.where(core == 0, r[0:1], r[1:2]) for r in rows]
-    table = jnp.concatenate(rows, axis=0).astype(jnp.bfloat16)
+        send_f(j, half).start()
+    def wait_b(which):
+        blocks = half if which else half - 1
+        await_bytes(shares(blocks, n_aux - 1), b_send.at[0], b_recv.at[which]).wait_recv()
+
+    wait_b(0)
     pair_row = lax.broadcasted_iota(jnp.int32, (LANE, block), 0)
     column = lax.broadcasted_iota(jnp.int32, (LANE, block), 1)
-    for j in range(n_pair):
-        pick = pair_row == jnp.where(column < rank, 2 * j, 2 * j + 1)
-        pick = jnp.where(pick, 1.0, 0.0).astype(jnp.bfloat16)
-        wt[j] = jnp.dot(table, pick, preferred_element_type=jnp.float32)
-
-    def collect_rows(i):
+
+    def spread_weights(side, start):
+        rows = [
+            ab[start + t, block : block + 16, :LANE].astype(jnp.float32) for t in range(half)
+        ]
+        rows = [jnp.where(core == 0, r[0:1], r[1:2]) for r in rows]
+        rows = rows + [jnp.zeros((half, LANE), jnp.float32)]
+        table = jnp.concatenate(rows, axis=0).astype(jnp.bfloat16)
+        for j in range(n_pair):
+            pick = pair_row == jnp.where(column < rank, 2 * j, 2 * j + 1)
+            pick = jnp.where(pick, 1.0, 0.0).astype(jnp.bfloat16)
+            wt[side, j] = jnp.dot(table, pick, preferred_element_type=jnp.float32)
+
+    spread_weights(0, near)
+    def collect_rows(i, part):
         for side in range(2):
             @pl.when(core == side)
             def _():
-                left_rows[i] = xb[i, side * rank : (side + 1) * rank, :]
+                left_rows[i, :, part] = xb[i, side * rank : (side + 1) * rank, part]
 
     def join(pieces):
         return jnp.concatenate(pieces, axis=0) if len(pieces) > 1 else pieces[0]
 
-    def turned(indices, blocks):
-        rows = join([left_rows[i] for i in indices])
-        columns = join([xb[j] for j in blocks])
-        products = lax.dot_general(
+    def gram(indices, blocks, part):
+        rows = join([left_rows[i, :, part] for i in indices])
+        columns = join([xb[j, :, part] for j in blocks])
+        return lax.dot_general(
             rows, columns, (((1,), (1,)), ((), ())), preferred_element_type=jnp.float32
         )
+
+    def weight(i, side, j):
+        return wt[side, j, pl.ds(i - (far if side else near), 1), :]
+
+    def turned(gram_rows, indices, sides, blocks):
         total = None
         for m, j in enumerate(blocks):
-            part = products[:, m * block : (m + 1) * block]
+            part = gram_rows[:, m * block : (m + 1) * block]
             scaled = [
-                part[k * rank : (k + 1) * rank] * wt[j, pl.ds(i, 1), :]
-                for k, i in enumerate(indices)
+                part[k * rank : (k + 1) * rank] * weight(i, side, j)
+                for k, (i, side) in enumerate(zip(indices, sides))
             ]
             turn = jnp.dot(
                 join(scaled).astype(jnp.bfloat16), ab[j, :block, :],
@@ -368,99 +382,107 @@
             total = turn if total is None else total + turn
         return total
 
-    def couple(indices, blocks, first=False):
-        turn = turned(indices, blocks)
+    def add_rows(turn, indices, fresh=False):
         for k, i in enumerate(indices):
             rows = turn[k * rank : (k + 1) * rank]
-            if first:
+            if fresh:
                 acc[i, :rank, :] = rows
             else:
                 acc[i, :rank, :] += rows
 
+    one = slice(0, first)
+    two = slice(first, first + base)
+    whole = slice(0, first + base)
     near_all = [near + t for t in range(half)]
+    await_bytes(
+        xb.at[pl.ds(0, half), :, mate_lanes], f_send.at[0], f_recv.at[half]
+    ).wait_recv()
     for t in range(half):
-        wait_f(near_peer(t))
-        collect_rows(near_peer(t))
+        collect_rows(near_peer(t), whole)
     for t in range(half):
-        couple(near_all, [near + t], first=t == 0)
-
-    def send_p(which, t, u):
+        turn = turned(gram(near_all, [near + t], whole), near_all, [0] * half, [near + t])
+        add_rows(turn, near_all, fresh=t == 0)
+    wait_b(1)
+    spread_weights(1, far)
+    def send_p(which, t, v):
         peer = near_peer(t)
-        other = lax.rem(chip + u, n_chip)
+        other = lax.rem(aux + v, n_aux)
         i = far_peer(t) if which else peer
         return remote(
-            parts.at[i, other], parts_in.at[which, t, u], p_send.at[which, t, u],
-            p_recv.at[which, t, u], peer, 2 * other + core,
-        )
-
-    hops = [(t, u) for t in range(half) for u in range(n_chip) if t or u]
+            parts.at[i, other], parts_in.at[which, t * n_aux + v], p_send.at[0],
+            p_recv.at[which], peer, other,
+        )
+
+    hops = [(t, v) for t in range(half) for v in range(n_aux) if t or v]
 
     def spread(which):
         for t in range(half):
             i = far_peer(t) if which else near_peer(t)
             for k in range(n_aux):
                 rows = acc[i, quarter * k : quarter * k + padded, :]
-                parts[i, k // 2, (k % 2) * padded : (k % 2 + 1) * padded, :] = rows.astype(
-                    parts.dtype
-                )
-            for u in range(n_chip):
-                if t or u:
-                    send_p(which, t, u).start()
+                parts[i, k] = rows.astype(parts.dtype)
+            for v in range(n_aux):
+                if t or v:
+                    send_p(which, t, v).start()
 
     for k in range(half):
         e = far_peer((half - k) % half)
         earlier = [far_peer((half - m) % half) for m in range(k)]
+        blocks = near_all + earlier + [e]
+        others = earlier + near_all
+        sides = [1] * k + [0] * half
+        width = block * len(blocks)
+        height = rank * len(others)
         wait_x(e)
-        send_f(e).start()
-        wait_f(e)
-        collect_rows(e)
-
-        couple([e], near_all + earlier + [e], first=True)
-        if earlier:
-            couple(earlier, [e])
-        if k == half - 1:
+        send_f(e, k).start()
+        collect_rows(e, one)
+        products[:, :width] = gram([e], blocks, one)
+        turned_products[:height, :] = gram(others, [e], one)
+        wait_f(k)
+        collect_rows(e, two)
+        full = products[:, :width] + gram([e], blocks, two)
+        add_rows(turned(full, [e], [1], blocks), [e], fresh=True)
+        if k < half - 1:
+            full = turned_products[:height, :] + gram(others, [e], two)
+            add_rows(turned(full, others, sides, [e]), others)
+        else:
+            middle = rank * k
+            full = turned_products[:middle, :] + gram(earlier, [e], two)
+            add_rows(turned(full, earlier, [1] * k, [e]), earlier)
             spread(1)
-        couple(near_all, [e])
+            full = turned_products[middle:height, :] + gram(near_all, [e], two)
+            add_rows(turned(full, near_all, [0] * half, [e]), near_all)
     spread(0)
 
     def collect(which):
         i = across if which else me
-        total = parts[i, chip].astype(jnp.float32)
-        for t, u in hops:
-            send_p(which, t, u).wait_recv()
-            total = total + parts_in[which, t, u].astype(jnp.float32)
-        ends[which] = total.astype(ends.dtype)
-
-    def send_q(k):
-        return remote(
-            ends.at[1, pl.ds(k * padded, padded)], ends_in.at[1, core],
-            q_send.at[k], q_recv.at[1, core], across, 2 * chip + k,
-        )
-
-    def mate_q():
-        return remote(
-            ends.at[0, pl.ds(pl.multiple_of((1 - core) * padded, padded), padded)],
-            ends_in.at[0, core], q_send.at[2], q_recv.at[0, core], me, mate,
-        )
-
-    collect(1)
-    for k in range(2):
-        send_q(k).start()
-    collect(0)
-    mate_q().start()
-    ends_in[0, core] = ends[0, pl.ds(pl.multiple_of(core * padded, padded), padded), :]
-
-    def arrive(which, side):
-        remote(
-            ends.at[which, pl.ds(0, padded)], ends_in.at[which, side],
-            q_send.at[0], q_recv.at[which, side], me, mate,
+        same = parts[i, aux].astype(jnp.float32)
+        cross = jnp.zeros_like(same)
+        await_bytes(
+            parts_in.at[which, pl.ds(1, len(hops))], p_send.at[0], p_recv.at[which]
         ).wait_recv()
-
-    arrive(0, 1 - core)
+        for t, v in hops:
+            got = parts_in[which, t * n_aux + v].astype(jnp.float32)
+            if v % 2 == 0:
+                same = same + got
+            else:
+                cross = cross + got
+        return same, cross
+
+    def send_q():
+        return remote(ends, ends_in, q_send.at[0], q_recv.at[0], across, aux)
+
+    same, cross = collect(1)
+    ends[core] = same.astype(ends.dtype)
+    ends[1 - core] = cross.astype(ends.dtype)
+    send_q().start()
+    same, cross = collect(0)
+    nears[core] = same
+    nears[1 - core] = cross
+    send_q().wait_recv()
+    at = lax.broadcasted_iota(jnp.int32, (padded, LANE), 0) + aux * quarter
     for side in range(2):
-        arrive(1, side)
-        total = ends_in[0, side].astype(jnp.float32) + ends_in[1, side].astype(jnp.float32)
-        at = lax.broadcasted_iota(jnp.int32, (padded, LANE), 0) + aux * quarter
+        total = nears[side] + ends_in[side].astype(jnp.float32)
         for s in range(2):
             part = total[:, s * LANE : (s + 1) * LANE]
             part = jnp.where(at < rank_ref[side], part, 0.0)
@@ -468,18 +490,12 @@
             for r in range(quarter):
                 out_ref[side, s : s + 1, r * rank : (r + 1) * rank] = part[r : r + 1, :rank]
 
-    for t in range(half):
-        send_a(t).wait_send()
-        send_x(far_peer(t)).wait_send()
-        if t:
-            pass_a(t).wait_send()
-            send_x(near_peer(t)).wait_send()
-    for t in range(1, n_pair):
-        j = lax.rem(me + n_pair - t, n_pair)
-        send_f(j).wait_send()
-        for u in range(1, n_aux):
-            send_b(j, u).wait_send()
-    own_f().wait_send()
+    await_bytes(shares(2 * half - 1, 1), a_send.at[0], a_recv.at[0]).wait_send()
+    await_bytes(
+        xb.at[pl.ds(0, n_pair - 1), :, lanes], x_send.at[0], x_recv.at[me]
+    ).wait_send()
+    await_bytes(xb.at[:, :, lanes], f_send.at[0], f_recv.at[0]).wait_send()
+    await_bytes(shares(n_pair - 1, n_aux - 1), b_send.at[0], b_recv.at[0]).wait_send()
     for level in range(extra):
         @pl.when(holder(core, level) != me)
         def _():
@@ -487,14 +503,11 @@
     if extra:
         @pl.when(self_holds)
         def _():
-            for j in range(n_pair):
-                send_g(j).wait_send()
-    for which in range(2):
-        for t, u in hops:
-            send_p(which, t, u).wait_send()
-    for k in range(2):
-        send_q(k).wait_send()
-    mate_q().wait_send()
+            send_g().wait_send()
+    await_bytes(
+        parts_in.at[:, pl.ds(1, len(hops))], p_send.at[0], p_recv.at[0]
+    ).wait_send()
+    send_q().wait_send()
 
 
 def own_amplitudes(rank, me, amp_v, fock_v, lmo_ref, neighbour_ref, rank_ref, a_ref):
@@ -561,38 +574,44 @@
     loads = 2 if tiles % 2 == 0 else 1
     dma = pltpu.SemaphoreType.DMA
     bf16 = jnp.bfloat16
-    anywhere = pl.BlockSpec(memory_space=pl.ANY)
-    scalars = pl.BlockSpec(memory_space=pltpu.SMEM)
     return pl.pallas_call(
         functools.partial(kernel, n_pair, n_aux, rank),
         out_shape=jax.ShapeDtypeStruct((2, 2, rank // n_aux * rank), jnp.float32),
-        in_specs=[anywhere] * 4 + [scalars] * 5,
+        in_specs=[pl.BlockSpec(memory_space=pl.ANY)] * 9,
         out_specs=pl.BlockSpec(memory_space=pltpu.VMEM),
         scratch_shapes=[
             pltpu.VMEM(x_own.shape, bf16),
             pltpu.VMEM(amplitudes.shape, bf16),
             pltpu.VMEM(energy.shape, jnp.float32),
             pltpu.VMEM(fock.shape, jnp.float32),
+            pltpu.SMEM(occ.shape, jnp.float32),
+            pltpu.SMEM(frequency.shape, jnp.float32),
+            pltpu.SMEM(lmo.shape, jnp.int32),
+            pltpu.SMEM(neighbours.shape, jnp.int32),
+            pltpu.SMEM(ranks.shape, jnp.int32),
             pltpu.VMEM(a_shape, bf16),
             pltpu.VMEM((2, 2, tall, LANE), jnp.float32),
             pltpu.VMEM((n_pair, block, depth), bf16),
             pltpu.VMEM((n_pair,) + a_shape, bf16),
-            pltpu.VMEM((n_pair, n_pair, block), jnp.float32),
+            pltpu.VMEM((2, n_pair, n_pair, block), jnp.float32),
+            pltpu.VMEM((rank, n_pair * block), jnp.float32),
+            pltpu.VMEM(((n_pair - 1) * rank, block), jnp.float32),
             pltpu.VMEM((n_pair, rank, depth), bf16),
             pltpu.VMEM((n_pair, tall, wide), jnp.float32),
-            pltpu.VMEM((n_pair, n_chip, 2 * padded, wide), bf16),
-            pltpu.VMEM((2, half, n_chip, 2 * padded, wide), bf16),
-            pltpu.VMEM((2, 2 * padded, wide), bf16),
-            pltpu.VMEM((2, 2, padded, wide), bf16),
-            dma((loads,)), dma((3,)), dma((3,)),
-            dma((n_pair,)), dma((n_pair,)),
-            dma((extra,)), dma((n_pair,)),
-            dma((n_pair,)), dma((n_pair,)),
-            dma((n_pair,)), dma((n_pair,)),
-            dma((n_pair,)), dma((n_pair,)),
-            dma((n_pair, n_aux)), dma((n_aux, n_pair)),
-            dma((2, half, n_chip)), dma((2, half, n_chip)),
-            dma((3,)), dma((2, 2)),
+            pltpu.VMEM((n_pair, n_aux, padded, wide), bf16),
+            pltpu.VMEM((2, half * n_aux, padded, wide), bf16),
+            pltpu.VMEM((2, padded, wide), bf16),
+            pltpu.VMEM((2, padded, wide), bf16),
+            pltpu.VMEM((2, padded, wide), jnp.float32),
+            dma((loads,)), dma((8,)), dma((3,)),
+            dma((1,)), dma((n_pair,)),
+            dma((extra,)), dma((1,)),
+            dma((1,)), dma((half + 1,)),
+            dma((1,)), dma((1,)),
+            dma((1,)), dma((3,)),
+            dma((1,)), dma((2,)),
+            dma((1,)), dma((2,)),
+            dma((1,)), dma((1,)),
         ],
         compiler_params=pltpu.CompilerParams(collective_id=0, has_side_effects=True),
     )(x_own, amplitudes, energy, fock, occ, frequency, lmo, neighbours, ranks)

time: 51.3 us -> 47.5 us (0.926)
  Pallas kernels: 48.9 us -> 45 us
    pallas_call x1, Pallas kernels: 48.9 us -> 45 us  [fused_coupling(): pl.pallas_call(functools.partial(kernel, n_pair, n_aux, rank), out_shape=...]
where the time goes in v2:
time: 47.5 us; the launch traced here: 47.1 us
  Pallas kernels  45 us (95%)
  other arithmetic  1.48 us (3%)
  between operations  0.68 us (1%)
    pallas_call x1, Pallas kernels, fused_coupling(): pl.pallas_call(functools.partial(kernel, n_pair, n_aux, rank), out_shape=...  45 us
    add x1, other arithmetic, kernel_body(): return drive + coupled  1.48 us

profile of v2, /device:TPU:0, one launch (start us, length us, event | category | flops | bytes accessed | tf_op | source)
XLA Modules:
  0.0 47.1 jit_solution(4839093916852552120)
XLA Ops:
  0.0 0.0 copy-start
  0.7 45.0 %shard_map.100 = f32[2,2,3600]{2,1,0:T(2,128)} custom-call(bf16[240,2304]{1,0:T(8,128)(2,1)} %bitcast.2, bf16[2,2,120,120]{3,2,1,0:T(8,128)(2,1)} %amp_hbm.1, f32[2,120]{1,0:T(2,128)} %energy_hbm.1, f32[32,32]{1,0:T(8,128)} %fock_hbm.1, f32[32]{0:T(128)} %occ_hbm.1, f32[1]{0:T(128)S(6)} %copy.11.frequency_hbm, s32[2,16]{1,0:T(2,128)} %bitcast.3, ...), custom_call_target="tpu_custom_call" | custom-call | tf_op jit(solution)/shard_map/pallas_call | solution.py:577
  45.7 0.0 copy-done
  45.7 1.5 %add.3 = f32[2,2,3600]{2,1,0:T(2,128)} add(f32[2,2,3600]{2,1,0:T(2,128)S(1)} %copy-done, f32[2,2,3600]{2,1,0:T(2,128)} %shard_map.100) | non-fusion elementwise | flops 14400 | bytes 172800 | tf_op jit(solution)/shard_map/add | solution.py:661
Async XLA Ops:
  0.0 45.7 %copy-start = (f32[2,2,3600]{2,1,0:T(2,128)S(1)}, f32[2,2,3600]{2,1,0:T(2,128)}, u32[]{:S(2)}) copy-start(f32[2,2,3600]{2,1,0:T(2,128)} %param.12) | copy-start | bytes 172804

commit v3 on v2

--- a/solution.py
+++ b/solution.py
@@ -126,6 +126,37 @@
         lanes = pl.ds(s * piece, piece)
         return pltpu.make_async_copy(x_hbm.at[:, lanes], xv.at[:, lanes], load_sem.at[s])
 
+    barrier = pltpu.get_barrier_semaphore()
+
+    def greet(pair, other):
+        pl.semaphore_signal(
+            barrier, inc=1, device_id=(pair, other), device_id_type=pl.DeviceIdType.MESH
+        )
+
+    def near_peer(t):
+        return near + lax.rem(spot_me + t, half)
+
+    def far_peer(t):
+        return far + lax.rem(spot_me + t, half)
+
+    turns = [3, 1, 2, 0]
+
+    def partner(t):
+        mask = turns[t] if half == len(turns) else t
+        return far + jnp.bitwise_xor(spot_me, mask)
+
+    def row(u):
+        return 2 * lax.rem(chip + u, n_chip) + core
+
+    for t in range(half):
+        greet(far_peer(t), aux)
+    for t in range(1, half):
+        greet(near_peer(t), aux)
+        for v in range(1, n_aux):
+            greet(near_peer(t), lax.rem(aux + v, n_aux))
+    for t in range(1, n_aux):
+        greet(me, lax.rem(aux + t, n_aux))
+
     smalls = [
         pltpu.make_async_copy(source, target, small_sem.at[s])
         for s, (source, target) in enumerate([
@@ -139,31 +170,6 @@
     for s in range(loads):
         load_x(s).start()
 
-    barrier = pltpu.get_barrier_semaphore()
-
-    def greet(pair, other):
-        pl.semaphore_signal(
-            barrier, inc=1, device_id=(pair, other), device_id_type=pl.DeviceIdType.MESH
-        )
-
-    def near_peer(t):
-        return near + lax.rem(spot_me + t, half)
-
-    def far_peer(t):
-        return far + lax.rem(spot_me + t, half)
-
-    def row(u):
-        return 2 * lax.rem(chip + u, n_chip) + core
-
-    for t in range(half):
-        greet(far_peer(t), aux)
-    for t in range(1, half):
-        greet(near_peer(t), aux)
-        for v in range(1, n_aux):
-            greet(near_peer(t), lax.rem(aux + v, n_aux))
-    for t in range(1, n_aux):
-        greet(me, lax.rem(aux + t, n_aux))
-
     def holder(which, level):
         return half // 2 * (1 + level) + which
 
@@ -279,7 +285,7 @@
     @pl.when(inner)
     def _():
         for t in range(half):
-            send_x(far_peer(t)).start()
+            send_x(partner(t)).start()
 
     own_f().start()
     mine_x.start()
@@ -297,7 +303,7 @@
     @pl.when(jnp.logical_not(inner))
     def _():
         for t in range(half):
-            send_x(far_peer(t)).start()
+            send_x(partner(t)).start()
 
     wait_a(1)
     for t in range(1, half):
@@ -368,19 +374,15 @@
         return wt[side, j, pl.ds(i - (far if side else near), 1), :]
 
     def turned(gram_rows, indices, sides, blocks):
-        total = None
-        for m, j in enumerate(blocks):
-            part = gram_rows[:, m * block : (m + 1) * block]
-            scaled = [
-                part[k * rank : (k + 1) * rank] * weight(i, side, j)
-                for k, (i, side) in enumerate(zip(indices, sides))
-            ]
-            turn = jnp.dot(
-                join(scaled).astype(jnp.bfloat16), ab[j, :block, :],
-                preferred_element_type=jnp.float32,
-            )
-            total = turn if total is None else total + turn
-        return total
+        scaled = []
+        for k, (i, side) in enumerate(zip(indices, sides)):
+            weights = [weight(i, side, j) for j in blocks]
+            weights = jnp.concatenate(weights, axis=1) if len(blocks) > 1 else weights[0]
+            scaled.append(gram_rows[k * rank : (k + 1) * rank] * weights)
+        return jnp.dot(
+            join(scaled).astype(jnp.bfloat16), join([ab[j, :block, :] for j in blocks]),
+            preferred_element_type=jnp.float32,
+        )
 
     def add_rows(turn, indices, fresh=False):
         for k, i in enumerate(indices):
@@ -409,7 +411,7 @@
         other = lax.rem(aux + v, n_aux)
         i = far_peer(t) if which else peer
         return remote(
-            parts.at[i, other], parts_in.at[which, t * n_aux + v], p_send.at[0],
+            parts.at[i, other], parts_in.at[which, t * n_aux + v], p_send.at[which],
             p_recv.at[which], peer, other,
         )
 
@@ -421,37 +423,42 @@
             for k in range(n_aux):
                 rows = acc[i, quarter * k : quarter * k + padded, :]
                 parts[i, k] = rows.astype(parts.dtype)
-            for v in range(n_aux):
-                if t or v:
-                    send_p(which, t, v).start()
+            if which:
+                for v in range(n_aux):
+                    if t or v:
+                        send_p(which, t, v).start()
+        if not which:
+            await_bytes(
+                parts_in.at[1, pl.ds(1, len(hops))], p_send.at[1], p_recv.at[1]
+            ).wait_send()
+            for t, v in hops:
+                send_p(which, t, v).start()
 
     for k in range(half):
-        e = far_peer((half - k) % half)
-        earlier = [far_peer((half - m) % half) for m in range(k)]
+        e = partner(k)
+        earlier = [partner(m) for m in range(k)]
         blocks = near_all + earlier + [e]
-        others = earlier + near_all
-        sides = [1] * k + [0] * half
+        prompt = k < half - 2
+        others = earlier + (near_all if prompt else [])
+        sides = [1] * k + ([0] * half if prompt else [])
         width = block * len(blocks)
         height = rank * len(others)
         wait_x(e)
         send_f(e, k).start()
         collect_rows(e, one)
         products[:, :width] = gram([e], blocks, one)
-        turned_products[:height, :] = gram(others, [e], one)
+        if others:
+            turned_products[:height, :] = gram(others, [e], one)
         wait_f(k)
         collect_rows(e, two)
         full = products[:, :width] + gram([e], blocks, two)
         add_rows(turned(full, [e], [1], blocks), [e], fresh=True)
-        if k < half - 1:
+        if others:
             full = turned_products[:height, :] + gram(others, [e], two)
             add_rows(turned(full, others, sides, [e]), others)
-        else:
-            middle = rank * k
-            full = turned_products[:middle, :] + gram(earlier, [e], two)
-            add_rows(turned(full, earlier, [1] * k, [e]), earlier)
-            spread(1)
-            full = turned_products[middle:height, :] + gram(near_all, [e], two)
-            add_rows(turned(full, near_all, [0] * half, [e]), near_all)
+    spread(1)
+    held = [partner(m) for m in range(half - 2, half)]
+    add_rows(turned(gram(near_all, held, whole), near_all, [0] * half, held), near_all)
     spread(0)
 
     def collect(which):
@@ -459,7 +466,7 @@
         same = parts[i, aux].astype(jnp.float32)
         cross = jnp.zeros_like(same)
         await_bytes(
-            parts_in.at[which, pl.ds(1, len(hops))], p_send.at[0], p_recv.at[which]
+            parts_in.at[which, pl.ds(1, len(hops))], p_send.at[which], p_recv.at[which]
         ).wait_recv()
         for t, v in hops:
             got = parts_in[which, t * n_aux + v].astype(jnp.float32)
@@ -505,7 +512,7 @@
         def _():
             send_g().wait_send()
     await_bytes(
-        parts_in.at[:, pl.ds(1, len(hops))], p_send.at[0], p_recv.at[0]
+        parts_in.at[0, pl.ds(1, len(hops))], p_send.at[0], p_recv.at[0]
     ).wait_send()
     send_q().wait_send()
 
@@ -610,7 +617,7 @@
             dma((1,)), dma((1,)),
             dma((1,)), dma((3,)),
             dma((1,)), dma((2,)),
-            dma((1,)), dma((2,)),
+            dma((2,)), dma((2,)),
             dma((1,)), dma((1,)),
         ],
         compiler_params=pltpu.CompilerParams(collective_id=0, has_side_effects=True),
@@ -627,7 +634,10 @@
         and rank % 8 == 0
         and rank % n_aux == 0
         and n_aux % 2 == 0
-        and n_pair % 2 == 0
+        and n_pair >= 8
+        and n_pair & (n_pair - 1) == 0
+        and rank <= LANE
+        and extra <= 2
         and 2 * n_pair <= LANE
         and tiles >= n_pair
         and (extra == 0 or n_pair % (2 * extra) == 0)

time: 47.5 us -> 46.8 us (0.985)
  Pallas kernels: 45 us -> 44.4 us
    pallas_call x1, Pallas kernels: 45 us -> 44.4 us  [fused_coupling(): pl.pallas_call(functools.partial(kernel, n_pair, n_aux, rank), out_shape=...]
where the time goes in v3:
time: 46.8 us; the launch traced here: 46.6 us
  Pallas kernels  44.4 us (95%)
  other arithmetic  1.48 us (3%)
  between operations  0.68 us (1%)
    pallas_call x1, Pallas kernels, fused_coupling(): pl.pallas_call(functools.partial(kernel, n_pair, n_aux, rank), out_shape=...  44.4 us
    add x1, other arithmetic, kernel_body(): return drive + coupled  1.48 us

profile of v3, /device:TPU:0, one launch (start us, length us, event | category | flops | bytes accessed | tf_op | source)
XLA Modules:
  0.0 46.6 jit_solution(6802670152157721683)
XLA Ops:
  0.0 0.0 copy-start
  0.7 44.4 %shard_map.100 = f32[2,2,3600]{2,1,0:T(2,128)} custom-call(bf16[240,2304]{1,0:T(8,128)(2,1)} %bitcast.2, bf16[2,2,120,120]{3,2,1,0:T(8,128)(2,1)} %amp_hbm.1, f32[2,120]{1,0:T(2,128)} %energy_hbm.1, f32[32,32]{1,0:T(8,128)} %fock_hbm.1, f32[32]{0:T(128)} %occ_hbm.1, f32[1]{0:T(128)S(6)} %copy.11.frequency_hbm, s32[2,16]{1,0:T(2,128)} %bitcast.3, ...), custom_call_target="tpu_custom_call" | custom-call | tf_op jit(solution)/shard_map/pallas_call | solution.py:584
  45.1 0.0 copy-done
  45.1 1.5 %add.3 = f32[2,2,3600]{2,1,0:T(2,128)} add(f32[2,2,3600]{2,1,0:T(2,128)S(1)} %copy-done, f32[2,2,3600]{2,1,0:T(2,128)} %shard_map.100) | non-fusion elementwise | flops 14400 | bytes 172800 | tf_op jit(solution)/shard_map/add | solution.py:671
Async XLA Ops:
  0.0 45.1 %copy-start = (f32[2,2,3600]{2,1,0:T(2,128)S(1)}, f32[2,2,3600]{2,1,0:T(2,128)}, u32[]{:S(2)}) copy-start(f32[2,2,3600]{2,1,0:T(2,128)} %param.12) | copy-start | bytes 172804
